TPU v7x, 128 devices: a whole 4x4x4 slice. The times are simulated.
128 devices in a mesh: zero: 8 (over x, core), width: 16 (over z, y).
Axes of the slice: x: 4, y: 4, z: 4, core: 2. Of those that a mesh axis runs over, the one named last changes fastest.
Arguments:
- weight_query: float32 [8192, 8192], P('zero', 'width'), may hold values from -0.09375 to 0.09375
- smooth_query: float32 [8192, 8192], P('zero', 'width'), may hold values from -0.0625 to 0.0625
- weight_key: float32 [8192, 512], P('zero', 'width'), may hold values from -0.09375 to 0.09375
- smooth_key: float32 [8192, 512], P('zero', 'width'), may hold values from -0.0625 to 0.0625
- weight_value: float32 [8192, 512], P('zero', 'width'), may hold values from -0.09375 to 0.09375
- smooth_value: float32 [8192, 512], P('zero', 'width'), may hold values from -0.0625 to 0.0625
- norm_train: float32 [8192], P(('zero', 'width')), may hold values from 0.25 to 1.75
- norm_step: float32 [8192], P(('zero', 'width')), may hold values from -0.3 to 0.3
Outputs:
- final_query: bfloat16 [8192, 8192], P(None, 'width')
- final_key: bfloat16 [8192, 512], P(None, 'width')
- final_value: bfloat16 [8192, 512], P(None, 'width')
- factor_query: float32 [8192], P('width')
- factor_key: float32 [512], P('width')
- factor_value: float32 [512], P('width')
- serve_norm: bfloat16 [8192], replicated
- result_query: float32 [8192, 8192], P('zero', 'width')
- result_key: float32 [8192, 512], P('zero', 'width')
- result_value: float32 [8192, 512], P('zero', 'width')
All inputs are finite; a program needn't handle non-finite values. Where the computation divides by a largest or mean magnitude, that divisor is 1e-20 or more.
Results may differ from a plain program's by a relative error of at most 0.001.
Values may be sent and summed in bfloat16 or wider, within the bound.
A program may use at most 128 MiB of HBM per device.

v0:
```python
import jax
import jax.numpy as jnp
from jax import lax
from jax.sharding import Mesh
from jax.sharding import PartitionSpec as P

D_MODEL = 8192
ZERO = ("zero_0", "zero_1")
ZERO_WIDTH = ("zero_0", "zero_1", "width_0", "width_1")
WIDTH = ("width_0", "width_1")


keep_rate = 0.7


def copy_for_each(x, axis):
    count = lax.axis_size(axis)
    return lax.all_to_all(jnp.broadcast_to(x[None], (count, *x.shape)), axis, 0, 0, tiled=True)


def taken_together(x, axis):
    return copy_for_each(x, axis).sum(axis=0)


def in_one(arrays, axis):
    line, at, outs = (jnp.concatenate([a.reshape(-1) for a in arrays]), 0, [])
    total = taken_together(line, axis)
    for a in arrays:
        outs.append(total[at : at + a.size].reshape(a.shape))
        at += a.size
    return tuple(outs)


def sent_together(arrays, axis, dim, along):
    widths = [a.shape[along] for a in arrays]
    both = jnp.concatenate(arrays, axis=along)
    whole = lax.all_gather(both, axis, axis=dim, tiled=True)
    return tuple(jnp.split(whole, [sum(widths[:k]) for k in range(1, len(widths))], axis=along))


def joined_along(pieces, dim):
    shape = list(pieces.shape[1:])
    shape[dim] *= pieces.shape[0]
    return jnp.moveaxis(pieces, 0, dim).reshape(shape)


def all_blocks(x, axes, order):
    pieces = x[None]
    for k in order:
        pieces = lax.all_gather(pieces, axes[k], axis=0, tiled=True)
    held = [lax.axis_size(axes[k]) for k in reversed(order)]
    pieces = pieces.reshape(*held, *x.shape)
    turned = sorted(range(len(order)), key=lambda place: order[len(order) - 1 - place])
    return pieces.transpose(*turned, *range(len(order), pieces.ndim)).reshape(-1, *x.shape)


def gathered_by_axis(x, axes, order, dim):
    return joined_along(all_blocks(x, axes, order), dim)


def on_device(
    weight_query,
    smooth_query,
    weight_key,
    smooth_key,
    weight_value,
    smooth_value,
    norm_train,
    norm_step,
):
    result_query = keep_rate * smooth_query + (1.0 - keep_rate) * weight_query
    result_key = keep_rate * smooth_key + (1.0 - keep_rate) * weight_key
    result_value = keep_rate * smooth_value + (1.0 - keep_rate) * weight_value
    total_query, total_key, total_value = in_one(
        (
            jnp.sum(jnp.abs(result_query), axis=0),
            jnp.sum(jnp.abs(result_key), axis=0),
            jnp.sum(jnp.abs(result_value), axis=0),
        ),
        ZERO,
    )
    factor_query = total_query / D_MODEL
    factor_key = total_key / D_MODEL
    factor_value = total_value / D_MODEL
    narrow_query, narrow_key, narrow_value = (
        (result_query / factor_query).astype(jnp.bfloat16),
        (result_key / factor_key).astype(jnp.bfloat16),
        (result_value / factor_value).astype(jnp.bfloat16),
    )
    final_query, final_key, final_value = sent_together(
        (narrow_query, narrow_key, narrow_value), ZERO, 0, 1
    )
    serve_norm = gathered_by_axis(
        (norm_train + norm_step).astype(jnp.bfloat16), ZERO_WIDTH, (0, 2, 3, 1), 0
    )
    return (
        final_query,
        final_key,
        final_value,
        factor_query,
        factor_key,
        factor_value,
        serve_norm,
        result_query,
        result_key,
        result_value,
    )


def solution(mesh):
    split = Mesh(mesh.devices.reshape(4, 2, 4, 4), ("zero_0", "zero_1", "width_0", "width_1"))
    in_specs = (
        P(ZERO, WIDTH),
        P(ZERO, WIDTH),
        P(ZERO, WIDTH),
        P(ZERO, WIDTH),
        P(ZERO, WIDTH),
        P(ZERO, WIDTH),
        P(ZERO_WIDTH),
        P(ZERO_WIDTH),
    )
    out_specs = (
        P(None, WIDTH),
        P(None, WIDTH),
        P(None, WIDTH),
        P(WIDTH),
        P(WIDTH),
        P(WIDTH),
        P(),
        P(ZERO, WIDTH),
        P(ZERO, WIDTH),
        P(ZERO, WIDTH),
    )
    return jax.shard_map(
        on_device, mesh=split, in_specs=in_specs, out_specs=out_specs, check_vma=False
    )
```

profile of v0, /device:TPU:1, one launch (start us, length us, event | category | flops | bytes accessed | tf_op | source)
XLA Modules:
  0.0 105.2 jit_solution(480870810976301172)
XLA Ops:
  7.2 0.0 copy-start.5
  7.2 0.0 copy-start.6
  7.2 0.0 copy-start.3
  7.2 0.0 copy-start.4
  7.2 0.0 all-gather.4.cloned.1.call-start
  7.3 2.9 %abs_reduce_fusion = (f32[512]{0:T(512)S(1)}, f32[1024,512]{1,0:T(8,128)S(1)}) fusion(f32[1024,512]{1,0:T(8,128)} %param.8, f32[1024,512]{1,0:T(8,128)} %param.9), kind=kLoop, calls=%fused_computation.1 | loop fusion | flops 2620928 | bytes 6293504 | tf_op jit(solution)/shard_map/reduce_sum | solution.py:76
  10.2 0.0 copy-done.5
  10.2 0.0 copy-done.6
  10.2 0.0 copy-done.3
  10.2 0.0 copy-done.4
  10.2 0.0 copy-start
  10.2 0.2 abs_reduce_fusion.1
  10.4 0.0 copy-start.2
  10.4 0.1 pad_maximum_fusion.1
  10.5 10.3 %all_to_all.6 = f32[8,1,576]{2,1,0:T(1,128)S(1)} all-to-all(f32[8,1,576]{2,1,0:T(1,128)S(1)} %broadcast_in_dim.4), channel_id=1, replica_groups=mesh['zero_0'=4,'zero_1'=2,'width_0'=4,'width_1'=4] {'zero_0','zero_1'}, dimensions={0} | all-to-all | bytes 36864 | tf_op jit(solution)/shard_map/all_to_all | solution.py:18
  20.8 0.1 slice_multiply_fusion.2
  20.9 0.1 divide_convert_fusion.2
  21.0 0.2 copy.42
  21.1 0.1 divide_convert_fusion.1
  21.2 0.2 copy.43
  21.4 0.3 divide_convert_fusion
  21.7 0.0 copy-done
  21.7 0.0 copy-done.1
  21.7 0.0 copy-done.2
  21.7 0.0 copy-done.8
  21.7 0.0 copy-done.9
  21.8 0.0 copy-done.7
  21.8 0.0 copy-start.12
  21.8 0.0 copy-start.10
  21.8 0.0 copy-start.11
  21.8 1.2 %pad_maximum_fusion = bf16[1024,576]{1,0:T(8,128)(2,1)} fusion(bf16[1024,32]{1,0:T(8,128)(2,1)S(1)} %copy.43, bf16[1024,32]{1,0:T(8,128)(2,1)S(1)} %copy.42, bf16[1024,512]{1,0:T(8,128)(2,1)S(1)} %divide_convert_fusion), kind=kLoop, calls=%fused_computation.3 | loop fusion | flops 3538944 | bytes 2359296 | tf_op jit(solution)/shard_map/concatenate | solution.py:36
  23.0 0.0 all-gather.4.cloned.1.call-update
  23.1 0.0 copy-done.12
  23.1 0.6 dynamic-slice
  24.3 0.0 copy-done.10
  24.3 0.0 copy-done.11
  24.4 0.2 dynamic-update-slice
  24.6 6.9 %all-reduce = bf16[256]{0:T(256)(128)(2,1)S(1)} all-reduce(bf16[256]{0:T(256)(128)(2,1)S(1)} %dynamic-update-slice), channel_id=2, replica_groups=mesh['zero_0'=4,'zero_1'=2,'width_0'=4,'width_1'=4] {'zero_0'}, use_global_device_ids=true, to_apply=%add | all-reduce | flops 256 | bytes 1024
  31.5 0.1 reshape.37
  31.5 9.4 %all-gather.1 = bf16[4,4,64]{2,1,0:T(4,128)(2,1)S(1)} all-gather(bf16[1,4,64]{2,1,0:T(4,128)(2,1)S(1)} %reshape.37), channel_id=1, replica_groups=mesh['zero_0'=4,'zero_1'=2,'width_0'=4,'width_1'=4] {'width_0'}, dimensions={0}, use_global_device_ids=true | all-gather | bytes 2560 | tf_op jit(solution)/shard_map/all_gather | solution.py:50
  40.9 10.6 %all_gather.18 = bf16[64,64]{1,0:T(8,128)(2,1)S(1)} all-gather(bf16[16,64]{1,0:T(8,128)(2,1)S(1)} %bitcast.6), channel_id=1, replica_groups=mesh['zero_0'=4,'zero_1'=2,'width_0'=4,'width_1'=4] {'width_1'}, dimensions={0}, use_global_device_ids=true | all-gather | bytes 10240 | tf_op jit(solution)/shard_map/all_gather | solution.py:50
  51.5 7.8 %all_gather.19 = bf16[128,64]{1,0:T(8,128)(2,1)S(1)} all-gather(bf16[64,64]{1,0:T(8,128)(2,1)S(1)} %all_gather.18), channel_id=1, replica_groups=mesh['zero_0'=4,'zero_1'=2,'width_0'=4,'width_1'=4] {'zero_1'}, dimensions={0}, use_global_device_ids=true | all-gather | bytes 24576 | tf_op jit(solution)/shard_map/all_gather | solution.py:50
  59.3 0.7 reshape_reshape.3
  60.0 22.6 %all-gather.4.cloned.1.call-done = bf16[8192,576]{1,0:T(8,128)(2,1)} async-done(((bf16[1024,576]{1,0:T(8,128)(2,1)}), bf16[8192,576]{1,0:T(8,128)(2,1)}) %all-gather.4.cloned.1.call-update) | async-done | bytes 9437200 | tf_op jit(solution)/shard_map/all_gather | solution.py:37
  82.6 4.3 %fusion = (bf16[8192,32]{1,0:T(8,128)(2,1)S(1)}, bf16[8192,32]{1,0:T(8,128)(2,1)}) fusion(bf16[8192,576]{1,0:T(8,128)(2,1)} %all-gather.4.cloned.1.call-done), kind=kLoop, calls=%fused_computation.15 | loop fusion | bytes 2097152 | tf_op jit(solution)/shard_map/split | solution.py:38
  87.0 2.6 %copy.45 = bf16[8192,32]{0,1:T(8,128)(2,1)} copy(bf16[8192,32]{1,0:T(8,128)(2,1)} %get-tuple-element.77) | data formatting | bytes 1048576
  89.5 1.5 %copy.46 = bf16[8192,32]{0,1:T(8,128)(2,1)} copy(bf16[8192,32]{1,0:T(8,128)(2,1)S(1)} %get-tuple-element.76) | data formatting | bytes 1048576
  91.0 7.3 %split.12 = bf16[8192,512]{1,0:T(8,128)(2,1)} slice(bf16[8192,576]{1,0:T(8,128)(2,1)} %all-gather.4.cloned.1.call-done), slice={[0:8192], [0:512]} | slice | bytes 16777216 | tf_op jit(solution)/shard_map/split | solution.py:38
  (10 shorter events, 0.1 us)
Async XLA Ops:
  7.2 3.0 %copy-start.5 = (f32[1024,32]{0,1:T(8,128)S(1)}, f32[1024,32]{0,1:T(8,128)}, u32[]{:S(2)}) copy-start(f32[1024,32]{0,1:T(8,128)} %param.10) | copy-start | bytes 393220
  7.2 3.0 %copy-start.6 = (f32[1024,32]{0,1:T(8,128)S(1)}, f32[1024,32]{0,1:T(8,128)}, u32[]{:S(2)}) copy-start(f32[1024,32]{0,1:T(8,128)} %param.11) | copy-start | bytes 393220
  7.2 3.0 %copy-start.3 = (f32[1024,32]{0,1:T(8,128)S(1)}, f32[1024,32]{0,1:T(8,128)}, u32[]{:S(2)}) copy-start(f32[1024,32]{0,1:T(8,128)} %param.12) | copy-start | bytes 393220
  7.2 3.0 %copy-start.4 = (f32[1024,32]{0,1:T(8,128)S(1)}, f32[1024,32]{0,1:T(8,128)}, u32[]{:S(2)}) copy-start(f32[1024,32]{0,1:T(8,128)} %param.13) | copy-start | bytes 393220
  7.2 75.4 %all-gather.4.cloned.1.call-start = ((), (), s32[]{:S(2)}) async-start(), calls=%async_computation.1 | async-start | bytes 11796480 | tf_op jit(solution)/shard_map/all_gather | solution.py:37
  10.2 11.5 %copy-start = (f32[1024,512]{1,0:T(8,128)}, f32[1024,512]{1,0:T(8,128)S(1)}, u32[]{:S(2)}) copy-start(f32[1024,512]{1,0:T(8,128)S(1)} %get-tuple-element.71) | copy-start | bytes 6291460
  10.4 11.3 %copy-start.1 = (f32[1024,32]{0,1:T(8,128)}, f32[1024,32]{0,1:T(8,128)S(1)}, u32[]{:S(2)}) copy-start(f32[1024,32]{0,1:T(8,128)S(1)} %get-tuple-element.75) | copy-start | bytes 393220
  10.4 11.3 %copy-start.2 = (f32[1024,32]{0,1:T(8,128)}, f32[1024,32]{0,1:T(8,128)S(1)}, u32[]{:S(2)}) copy-start(f32[1024,32]{0,1:T(8,128)S(1)} %get-tuple-element.81) | copy-start | bytes 393220
  20.9 0.9 copy-start.8
  20.9 0.9 copy-start.9
  20.9 0.9 copy-start.7
  21.8 1.3 %copy-start.12 = (u32[128]{0:T(128)S(1)}, u32[128]{0:T(128)}, u32[]{:S(2)}) copy-start(u32[128]{0:T(128)} %constant.18) | copy-start | bytes 1540
  21.8 2.5 %copy-start.10 = (f32[64]{0:T(128)S(1)}, f32[64]{0:T(128)}, u32[]{:S(2)}) copy-start(f32[64]{0:T(128)} %param.14) | copy-start | bytes 772
  21.8 2.5 %copy-start.11 = (f32[64]{0:T(128)S(1)}, f32[64]{0:T(128)}, u32[]{:S(2)}) copy-start(f32[64]{0:T(128)} %param.15) | copy-start | bytes 772
Sparse Core Ops, SparseCore 0:
  23.2 59.3 all-gather.3
where the time goes:
time: 105 us
  blocking collectives  44.8 us (43%)
  waiting for transfers between devices  22.6 us (22%)
  local copies, waits for them, and re-layouts  17.8 us (17%)
  between operations  14.9 us (14%)
  other arithmetic  4.97 us (5%)
    all_gather x3, blocking collectives, all_blocks(): pieces = lax.all_gather(pieces, axes[k], axis=0, tiled=True)  27.7 us
    all_gather x1, waiting for transfers between devices, sent_together(): whole = lax.all_gather(both, axis, axis=dim, tiled=True)  22.6 us
    split x2, local copies, waits for them, and re-layouts, sent_together(): jnp.split(whole, [sum(widths[:k]) for k in range(1, len(widths))], axis=a...  11.6 us
    all_to_all x1, blocking collectives, copy_for_each(): lax.all_to_all(jnp.broadcast_to(x[None], (count, *x.shape)), axis, 0, 0,...  10.3 us
    unnamed x1, blocking collectives  6.85 us
    unnamed x32, local copies, waits for them, and re-layouts  5.04 us
    reduce_sum x1, other arithmetic, on_device(): jnp.sum(jnp.abs(result_query), axis=0)  2.93 us
  transfers between devices with their start and end apart: 1, of which 1 were waited for; matrix products, arithmetic and copies ran while one was open for 2% of the time, Pallas kernels for 0%

commit v1 on v0

v1 whole, which is shorter than its diff:
```python
import jax
import jax.numpy as jnp
from jax import lax
from jax.experimental import pallas as pl
from jax.experimental.pallas import tpu as pltpu
from jax.sharding import Mesh
from jax.sharding import PartitionSpec as P

D_MODEL = 8192
ZERO = ("zero_0", "zero_1")
ZERO_WIDTH = ("zero_0", "zero_1", "width_0", "width_1")
WIDTH = ("width_0", "width_1")
MESH = pl.DeviceIdType.MESH

keep_rate = 0.7

ROWS = 1024
COLS = 512
HALF = ROWS // 2
KV = 64
LANES = 128
TILES = COLS // LANES
STEP = 128
KV_ROW, NORM_ROW = TILES, TILES + 1
SUM_ROWS = TILES + 2

UNITS = tuple((tile, half) for tile in range(TILES + 1) for half in range(2))


def mix(smooth, weight):
    return keep_rate * smooth + (1.0 - keep_rate) * weight


def gather_kernel(
    wq, sq, wk, sk, wv, sv, norm_a, norm_b,
    out_q, out_kv, res_q, res_kv, fac_q, fac_k, fac_v, norm_out,
    wq_v, sq_v, wkv_v, skv_v, inv, sums, norm_y, norm_z, norm_all,
    in_sem, sum_send, sum_recv, own_send, fwd_send, rel_send,
    side_recv, far_recv, rel_recv, norm_send, norm_recv,
):
    x, c = lax.axis_index("zero_0"), lax.axis_index("zero_1")
    z, y = lax.axis_index("width_0"), lax.axis_index("width_1")
    me = x * 2 + c
    right, left = lax.rem(x + 1, 4), lax.rem(x + 3, 4)
    sides = ((left, right), (right, left))

    loads = []

    def load(src, dst):
        copy = pltpu.make_async_copy(src, dst, in_sem.at[len(loads)])
        copy.start()
        loads.append(copy)

    for t in range(TILES):
        cols = pl.ds(t * LANES, LANES)
        load(wq.at[:, cols], wq_v.at[:, cols])
        load(sq.at[:, cols], sq_v.at[:, cols])
    load(wk, wkv_v.at[pl.ds(0, 32), :])
    load(sk, skv_v.at[pl.ds(0, 32), :])
    load(wv, wkv_v.at[pl.ds(32, 32), :])
    load(sv, skv_v.at[pl.ds(32, 32), :])

    def group_peer(d):
        other = lax.rem(me + d, 8)
        return {"zero_0": other // 2, "zero_1": lax.rem(other, 2)}

    barrier = pltpu.get_barrier_semaphore()
    for d in (4, 5, 3, 2, 6, 7, 1):
        pl.semaphore_signal(barrier, inc=1, device_id=group_peer(d), device_id_type=MESH)
    for d in (2, 1, 3):
        pl.semaphore_signal(barrier, inc=1, device_id={"width_1": lax.rem(y + d, 4)}, device_id_type=MESH)
        pl.semaphore_signal(barrier, inc=1, device_id={"width_0": lax.rem(z + d, 4)}, device_id_type=MESH)

    def sum_tile(t):
        loads[2 * t].wait()
        loads[2 * t + 1].wait()
        cols = pl.ds(t * LANES, LANES)

        def body(i, acc):
            rows = pl.ds(pl.multiple_of(i * STEP, STEP), STEP)
            r = mix(sq_v[rows, cols], wq_v[rows, cols])
            res_q[rows, cols] = r
            return acc + jnp.sum(jnp.abs(r).reshape(STEP // 8, 8, LANES), axis=0)

        acc = lax.fori_loop(0, ROWS // STEP, body, jnp.zeros((8, LANES), jnp.float32))
        sums[me, t] = jnp.sum(acc, axis=0, keepdims=True)

    def send_sums(first, count, which):
        for d in (4, 5, 3, 2, 6, 7, 1):
            pltpu.make_async_remote_copy(
                src_ref=sums.at[me, pl.ds(first, count)],
                dst_ref=sums.at[me, pl.ds(first, count)],
                send_sem=sum_send.at[which, d],
                recv_sem=sum_recv.at[which, d],
                device_id=group_peer(d),
                device_id_type=MESH,
            ).start()

    def sums_copy(first, count, which, d):
        other = lax.rem(me + 8 - d, 8)
        return pltpu.make_async_remote_copy(
            src_ref=sums.at[other, pl.ds(first, count)],
            dst_ref=sums.at[other, pl.ds(first, count)],
            send_sem=sum_send.at[which, d],
            recv_sem=sum_recv.at[which, d],
            device_id=group_peer(d),
            device_id_type=MESH,
        )

    lane_of = lax.broadcasted_iota(jnp.int32, (KV, LANES), 1)
    diagonal = lane_of == lax.broadcasted_iota(jnp.int32, (KV, LANES), 0)

    sum_tile(0)
    pl.semaphore_wait(barrier, 13)
    send_sums(0, 1, 0)
    for t in range(1, TILES):
        sum_tile(t)
    for copy in loads[2 * TILES :]:
        copy.wait()
    acc = jnp.zeros((KV, LANES), jnp.float32)
    for j in range(ROWS // LANES):
        cols = pl.ds(j * LANES, LANES)
        r = mix(skv_v[:, cols], wkv_v[:, cols])
        res_kv[:, cols] = r
        acc = acc + jnp.abs(r)
    row_sums = jnp.sum(acc, axis=1, keepdims=True)
    sums[me, KV_ROW] = jnp.sum(jnp.where(diagonal, row_sums, 0.0), axis=0, keepdims=True)
    own_norm = norm_a[...] + norm_b[...]
    sums[me, NORM_ROW] = jnp.concatenate([own_norm, own_norm], axis=1)
    send_sums(1, SUM_ROWS - 1, 1)

    def place(origin, k):
        tile, half = UNITS[k]
        if tile < TILES:
            rows = pl.ds(pl.multiple_of(origin * ROWS + half * HALF, HALF), HALF)
            return out_q.at[rows, pl.ds(tile * LANES, LANES)]
        return out_kv.at[:, pl.ds(pl.multiple_of(origin * ROWS + half * HALF, HALF), HALF)]

    def unit_copy(origin, k, send_sem, recv_sem, device):
        ref = place(origin, k)
        return pltpu.make_async_remote_copy(
            src_ref=ref, dst_ref=ref, send_sem=send_sem, recv_sem=recv_sem, device_id=device, device_id_type=MESH
        )

    partner = {"zero_1": 1 - c}
    to_right, to_left = {"zero_0": right}, {"zero_0": left}
    sends = []

    def send(copy):
        copy.start()
        sends.append(copy)

    def send_own(k):
        ways = [(0, to_right), (1, to_left)]
        for side, device in ways if UNITS[k][1] == 0 else ways[::-1]:
            send(unit_copy(me, k, own_send.at[side, k], side_recv.at[side, k], device))
        send(unit_copy(me, k, own_send.at[2, k], rel_recv.at[0, k], partner))

    def narrow_tile(t):
        total = sums[0, t]
        for other in range(1, 8):
            total = total + sums[other, t]
        factor = total * (1.0 / D_MODEL)
        if t < TILES:
            fac_q[:, pl.ds(t * LANES, LANES)] = factor
            scale = 1.0 / factor
        else:
            fac_k[...] = factor[:, 0:32]
            fac_v[...] = pltpu.roll(factor, LANES - 32, 1)[:, 0:32]
            spread = jnp.sum(jnp.where(diagonal, jnp.broadcast_to(factor, (KV, LANES)), 0.0), axis=1, keepdims=True)
            scale = 1.0 / jnp.broadcast_to(spread, (KV, LANES))
        for half in range(2):
            if t < TILES:
                cols = pl.ds(t * LANES, LANES)

                def body(i, carry):
                    at = half * HALF + i * STEP
                    rows = pl.ds(pl.multiple_of(at, STEP), STEP)
                    there = pl.ds(pl.multiple_of(me * ROWS + at, STEP), STEP)
                    out_q[there, cols] = (res_q[rows, cols] * scale).astype(jnp.bfloat16)
                    return carry

                lax.fori_loop(0, HALF // STEP, body, 0)
            else:
                for j in range(HALF // LANES):
                    at = half * HALF + j * LANES
                    there = pl.ds(pl.multiple_of(me * ROWS + at, LANES), LANES)
                    out_kv[:, there] = (res_kv[:, pl.ds(at, LANES)] * scale).astype(jnp.bfloat16)
            send_own(2 * t + half)

    for d in range(1, 8):
        sums_copy(0, 1, 0, d).wait_recv()
    narrow_tile(0)
    for d in range(1, 8):
        sums_copy(1, SUM_ROWS - 1, 1, d).wait_recv()
    for t in range(1, TILES + 1):
        narrow_tile(t)

    def norm_copy(buf, at, stage, d, axis, here):
        return pltpu.make_async_remote_copy(
            src_ref=buf.at[at],
            dst_ref=buf.at[at],
            send_sem=norm_send.at[stage, d],
            recv_sem=norm_recv.at[stage, d],
            device_id={axis: lax.rem(here + d, 4)},
            device_id_type=MESH,
        )

    for other in range(8):
        norm_y[y, pl.ds(other, 1), :] = sums[other, NORM_ROW]
    for d in (2, 1, 3):
        norm_copy(norm_y, y, 0, d, "width_1", y).start()

    def norm_along_z():
        for d in (1, 3, 2):
            norm_copy(norm_y, lax.rem(y + 4 - d, 4), 0, d, "width_1", y).wait_recv()
        low = lax.broadcasted_iota(jnp.int32, (8, LANES), 1) < 64
        norm_z[z, 0] = jnp.where(low, norm_y[0], norm_y[1])
        norm_z[z, 1] = jnp.where(low, norm_y[2], norm_y[3])
        for d in (2, 1, 3):
            norm_copy(norm_z, z, 1, d, "width_0", z).start()

    def norm_end():
        for d in (1, 3, 2):
            norm_copy(norm_z, lax.rem(z + 4 - d, 4), 1, d, "width_0", z).wait_recv()
        for zz in range(4):
            for pair in range(2):
                for other in range(8):
                    norm_all[pl.ds(other * 8 + zz * 2 + pair, 1), :] = norm_z[zz, pair, pl.ds(other, 1), :]
        norm_out[...] = norm_all[...].astype(jnp.bfloat16)
        for d in range(1, 4):
            norm_copy(norm_y, y, 0, d, "width_1", y).wait_send()
            norm_copy(norm_z, z, 1, d, "width_0", z).wait_send()

    far = lax.rem(x + 2, 4)
    for k in range(len(UNITS)):
        for side in range(2):
            origin = (left if side == 0 else right) * 2 + c
            unit_copy(origin, k, own_send.at[side, k], side_recv.at[side, k], to_right).wait_recv()
            if UNITS[k][1] == side:
                send(unit_copy(origin, k, fwd_send.at[k], far_recv.at[k], to_right if side == 0 else to_left))
            send(unit_copy(origin, k, rel_send.at[side, k], rel_recv.at[1 + side, k], partner))
        if k == 2:
            norm_along_z()
        if k == 4:
            norm_end()
    for k in range(len(UNITS)):
        unit_copy(far * 2 + c, k, fwd_send.at[k], far_recv.at[k], to_right).wait_recv()
        send(unit_copy(far * 2 + c, k, rel_send.at[2, k], rel_recv.at[3, k], partner))

    for d in range(1, 8):
        sums_copy(0, 1, 0, d).wait_send()
        sums_copy(1, SUM_ROWS - 1, 1, d).wait_send()
    for copy in sends:
        copy.wait_send()
    for which, origin in enumerate((x, left, right, far)):
        for k in range(len(UNITS)):
            unit_copy(origin * 2 + 1 - c, k, own_send.at[2, k], rel_recv.at[which, k], partner).wait_recv()


def write_kernel(
    out_q, out_kv, res_q, res_kv, fac_q, fac_k, fac_v, norm,
    final_q, final_k, final_v, factor_q, factor_k, factor_v, serve_norm, result_q, result_k, result_v, sem,
):
    copies = []

    def write(src, dst):
        copy = pltpu.make_async_copy(src, dst, sem.at[len(copies)])
        copy.start()
        copies.append(copy)

    for part in range(8):
        rows = pl.ds(part * ROWS, ROWS)
        write(out_q.at[rows, :], final_q.at[rows, :])
    write(res_q, result_q)
    write(out_kv.at[pl.ds(0, 32), :], final_k)
    write(out_kv.at[pl.ds(32, 32), :], final_v)
    write(res_kv.at[pl.ds(0, 32), :], result_k)
    write(res_kv.at[pl.ds(32, 32), :], result_v)
    write(fac_q, factor_q)
    write(fac_k, factor_k)
    write(fac_v, factor_v)
    write(norm, serve_norm)
    for copy in copies:
        copy.wait()


def on_device(weight_query, smooth_query, weight_key, smooth_key, weight_value, smooth_value, norm_train, norm_step):
    f32, bf16 = jnp.float32, jnp.bfloat16
    any_spec, vmem_spec = pl.BlockSpec(memory_space=pl.ANY), pl.BlockSpec(memory_space=pltpu.VMEM)
    held = (
        ((D_MODEL, COLS), bf16),
        ((KV, D_MODEL), bf16),
        ((ROWS, COLS), f32),
        ((KV, ROWS), f32),
        ((1, COLS), f32),
        ((1, 32), f32),
        ((1, 32), f32),
        ((64, LANES), bf16),
    )
    units = len(UNITS)
    dma = pltpu.SemaphoreType.DMA
    gathered = pl.pallas_call(
        gather_kernel,
        out_shape=tuple(pltpu.VMEM(shape, dtype) for shape, dtype in held),
        in_specs=[any_spec] * 6 + [vmem_spec] * 2,
        out_specs=tuple(vmem_spec for _ in held),
        scratch_shapes=[
            pltpu.VMEM((ROWS, COLS), f32),
            pltpu.VMEM((ROWS, COLS), f32),
            pltpu.VMEM((KV, ROWS), f32),
            pltpu.VMEM((KV, ROWS), f32),
            pltpu.VMEM((1, COLS), f32),
            pltpu.VMEM((8, SUM_ROWS, 1, LANES), f32),
            pltpu.VMEM((4, 8, LANES), f32),
            pltpu.VMEM((4, 2, 8, LANES), f32),
            pltpu.VMEM((64, LANES), f32),
            dma((2 * TILES + 4,)),
            dma((2, 8)),
            dma((2, 8)),
            dma((3, units)),
            dma((units,)),
            dma((3, units)),
            dma((2, units)),
            dma((units,)),
            dma((4, units)),
            dma((2, 4)),
            dma((2, 4)),
        ],
        compiler_params=pltpu.CompilerParams(
            collective_id=0, has_side_effects=True, vmem_limit_bytes=16 * 1024 * 1024
        ),
        name="gather",
    )(
        weight_query, smooth_query, weight_key.T, smooth_key.T, weight_value.T, smooth_value.T,
        norm_train.reshape(1, 64), norm_step.reshape(1, 64),
    )
    outs = (
        ((D_MODEL, COLS), bf16),
        ((32, D_MODEL), bf16),
        ((32, D_MODEL), bf16),
        ((1, COLS), f32),
        ((1, 32), f32),
        ((1, 32), f32),
        ((64, LANES), bf16),
        ((ROWS, COLS), f32),
        ((32, ROWS), f32),
        ((32, ROWS), f32),
    )
    fq, fk, fv, cq, ck, cv, norm, rq, rk, rv = pl.pallas_call(
        write_kernel,
        out_shape=tuple(jax.ShapeDtypeStruct(shape, dtype) for shape, dtype in outs),
        in_specs=[vmem_spec] * len(held),
        out_specs=tuple(any_spec for _ in outs),
        scratch_shapes=[dma((17,))],
        compiler_params=pltpu.CompilerParams(vmem_limit_bytes=4 * 1024 * 1024),
        name="write",
    )(*gathered)
    return (
        fq, fk.T, fv.T, cq.reshape(COLS), ck.reshape(32), cv.reshape(32), norm.reshape(D_MODEL), rq, rk.T, rv.T
    )


def solution(mesh):
    split = Mesh(mesh.devices.reshape(4, 2, 4, 4), ("zero_0", "zero_1", "width_0", "width_1"))
    in_specs = (
        P(ZERO, WIDTH),
        P(ZERO, WIDTH),
        P(ZERO, WIDTH),
        P(ZERO, WIDTH),
        P(ZERO, WIDTH),
        P(ZERO, WIDTH),
        P(ZERO_WIDTH),
        P(ZERO_WIDTH),
    )
    out_specs = (
        P(None, WIDTH),
        P(None, WIDTH),
        P(None, WIDTH),
        P(WIDTH),
        P(WIDTH),
        P(WIDTH),
        P(),
        P(ZERO, WIDTH),
        P(ZERO, WIDTH),
        P(ZERO, WIDTH),
    )
    return jax.shard_map(
        on_device, mesh=split, in_specs=in_specs, out_specs=out_specs, check_vma=False
    )
```

time: 105 us -> 67.4 us (0.64)
  Pallas kernels: 0 us -> 58.4 us
  blocking collectives: 44.8 us -> 0 us
  waiting for transfers between devices: 22.6 us -> 0 us
  between operations: 14.9 us -> 0.67 us
  local copies, waits for them, and re-layouts: 17.8 us -> 8.1 us
  other arithmetic: 4.97 us -> 0 us
    pallas_call x0 -> x2, Pallas kernels: none -> 58.4 us  [the longest x1 53.9 us: on_device(): pl.pallas_call(gather_kernel, out_shape=tuple((pltpu.VMEM(shape, dtype) f...]
    all_gather x3 -> x0, blocking collectives: 27.7 us -> none  [all_blocks(): pieces = lax.all_gather(pieces, axes[k], axis=0, tiled=True)]
    all_gather x1 -> x0, waiting for transfers between devices: 22.6 us -> none  [sent_together(): whole = lax.all_gather(both, axis, axis=dim, tiled=True)]
    split x2 -> x0, local copies, waits for them, and re-layouts: 11.6 us -> none  [sent_together(): jnp.split(whole, [sum(widths[:k]) for k in range(1, len(widths))], axis=a...]
    all_to_all x1 -> x0, blocking collectives: 10.3 us -> none  [copy_for_each(): lax.all_to_all(jnp.broadcast_to(x[None], (count, *x.shape)), axis, 0, 0,...]
    unnamed x1 -> x0, blocking collectives: 6.85 us -> none
    reduce_sum x3 -> x0, other arithmetic: 3.12 us -> none  [the longest x1 2.93 us: on_device(): jnp.sum(jnp.abs(result_query), axis=0)]
    unnamed x32 -> x16, local copies, waits for them, and re-layouts: 5.04 us -> 8.1 us
  transfers between devices with their start and end apart: 1 -> 0, of which waited for: 1 -> 0; matrix products, arithmetic and copies ran while one was open for 2% -> 0% of each run, Pallas kernels for 0% -> 0%
where the time goes in v1:
time: 67.4 us; the launch traced here: 67.1 us
  Pallas kernels  58.4 us (87%)
  local copies, waits for them, and re-layouts  8.1 us (12%)
    pallas_call x1, Pallas kernels, on_device(): pl.pallas_call(gather_kernel, out_shape=tuple((pltpu.VMEM(shape, dtype) f...  53.9 us
    unnamed x16, local copies, waits for them, and re-layouts  8.1 us
    pallas_call x1, Pallas kernels, on_device(): pl.pallas_call(write_kernel, out_shape=tuple((jax.ShapeDtypeStruct(shape,...  4.45 us

profile of v1, /device:TPU:1, one launch (start us, length us, event | category | flops | bytes accessed | tf_op | source)
XLA Modules:
  0.0 67.1 jit_solution(4126370270478266989)
XLA Ops:
  0.6 0.0 copy-start
  0.7 1.6 %copy-done = f32[1024,512]{1,0:T(8,128)S(1)} copy-done((f32[1024,512]{1,0:T(8,128)S(1)}, f32[1024,512]{1,0:T(8,128)}, u32[]{:S(2)}) %copy-start) | copy-done | bytes 2097176
  2.2 0.0 copy-start.1
  2.2 1.6 %copy-done.1 = f32[1024,512]{1,0:T(8,128)S(1)} copy-done((f32[1024,512]{1,0:T(8,128)S(1)}, f32[1024,512]{1,0:T(8,128)}, u32[]{:S(2)}) %copy-start.1) | copy-done | bytes 2097176
  3.8 0.0 copy-start.2
  3.8 0.9 %copy-done.2 = f32[1024,32]{0,1:T(8,128)S(1)} copy-done((f32[1024,32]{0,1:T(8,128)S(1)}, f32[1024,32]{0,1:T(8,128)}, u32[]{:S(2)}) %copy-start.2) | copy-done | bytes 131096
  4.7 0.0 copy-start.3
  4.7 0.9 %copy-done.3 = f32[1024,32]{0,1:T(8,128)S(1)} copy-done((f32[1024,32]{0,1:T(8,128)S(1)}, f32[1024,32]{0,1:T(8,128)}, u32[]{:S(2)}) %copy-start.3) | copy-done | bytes 131096
  5.6 0.0 copy-start.4
  5.6 0.9 %copy-done.4 = f32[1024,32]{0,1:T(8,128)S(1)} copy-done((f32[1024,32]{0,1:T(8,128)S(1)}, f32[1024,32]{0,1:T(8,128)}, u32[]{:S(2)}) %copy-start.4) | copy-done | bytes 131096
  6.5 0.0 copy-start.5
  6.5 0.9 %copy-done.5 = f32[1024,32]{0,1:T(8,128)S(1)} copy-done((f32[1024,32]{0,1:T(8,128)S(1)}, f32[1024,32]{0,1:T(8,128)}, u32[]{:S(2)}) %copy-start.5) | copy-done | bytes 131096
  7.4 0.0 copy-start.6
  7.5 0.7 copy-done.6
  8.1 0.0 copy-start.7
  8.1 0.7 copy-done.7
  8.8 53.9 %gather.1 = (bf16[8192,512]{1,0:T(8,128)(2,1)S(1)}, bf16[64,8192]{1,0:T(8,128)(2,1)S(1)}, f32[1024,512]{1,0:T(8,128)S(1)}, f32[64,1024]{1,0:T(8,128)S(1)}, f32[1...) custom-call(f32[1024,512]{1,0:T(8,128)S(1)} %copy-done, ...), custom_call_target="tpu_custom_call" | custom-call | tf_op jit(solution)/shard_map/gather/pallas_call | solution.py:303
  62.7 4.4 %write.1 = (bf16[8192,512]{1,0:T(8,128)(2,1)}, bf16[32,8192]{1,0:T(8,128)(2,1)}, bf16[32,8192]{1,0:T(8,128)(2,1)}, f32[1,512]{1,0:T(1,128)}, f32[1,32]{1,0:T(1,1...) custom-call(bf16[8192,512]{1,0:T(8,128)(2,1)S(1)} %get-tuple-element, ...), custom_call_target="tpu_custom_call" | custom-call | tf_op jit(solution)/shard_map/write/pallas_call | solution.py:350
Async XLA Ops:
  0.6 1.6 %copy-start = (f32[1024,512]{1,0:T(8,128)S(1)}, f32[1024,512]{1,0:T(8,128)}, u32[]{:S(2)}) copy-start(f32[1024,512]{1,0:T(8,128)} %wq.1) | copy-start | bytes 6291460
  2.2 1.6 %copy-start.1 = (f32[1024,512]{1,0:T(8,128)S(1)}, f32[1024,512]{1,0:T(8,128)}, u32[]{:S(2)}) copy-start(f32[1024,512]{1,0:T(8,128)} %sq.1) | copy-start | bytes 6291460
  3.8 0.9 %copy-start.2 = (f32[1024,32]{0,1:T(8,128)S(1)}, f32[1024,32]{0,1:T(8,128)}, u32[]{:S(2)}) copy-start(f32[1024,32]{0,1:T(8,128)} %param.10) | copy-start | bytes 393220
  4.7 0.9 %copy-start.3 = (f32[1024,32]{0,1:T(8,128)S(1)}, f32[1024,32]{0,1:T(8,128)}, u32[]{:S(2)}) copy-start(f32[1024,32]{0,1:T(8,128)} %param.11) | copy-start | bytes 393220
  5.6 0.9 %copy-start.4 = (f32[1024,32]{0,1:T(8,128)S(1)}, f32[1024,32]{0,1:T(8,128)}, u32[]{:S(2)}) copy-start(f32[1024,32]{0,1:T(8,128)} %param.12) | copy-start | bytes 393220
  6.5 0.9 %copy-start.5 = (f32[1024,32]{0,1:T(8,128)S(1)}, f32[1024,32]{0,1:T(8,128)}, u32[]{:S(2)}) copy-start(f32[1024,32]{0,1:T(8,128)} %param.13) | copy-start | bytes 393220
  7.4 0.7 copy-start.6
  8.1 0.7 copy-start.7

commit v2 on v1

--- a/solution.py
+++ b/solution.py
@@ -34,7 +34,7 @@
 def gather_kernel(
     wq, sq, wk, sk, wv, sv, norm_a, norm_b,
     out_q, out_kv, res_q, res_kv, fac_q, fac_k, fac_v, norm_out,
-    wq_v, sq_v, wkv_v, skv_v, inv, sums, norm_y, norm_z, norm_all,
+    wq_v, sq_v, wkv_v, skv_v, norm_v, sums, norm_y, norm_z, norm_all,
     in_sem, sum_send, sum_recv, own_send, fwd_send, rel_send,
     side_recv, far_recv, rel_recv, norm_send, norm_recv,
 ):
@@ -59,6 +59,8 @@
     load(sk, skv_v.at[pl.ds(0, 32), :])
     load(wv, wkv_v.at[pl.ds(32, 32), :])
     load(sv, skv_v.at[pl.ds(32, 32), :])
+    load(norm_a, norm_v.at[0])
+    load(norm_b, norm_v.at[1])
 
     def group_peer(d):
         other = lax.rem(me + d, 8)
@@ -125,7 +127,7 @@
         acc = acc + jnp.abs(r)
     row_sums = jnp.sum(acc, axis=1, keepdims=True)
     sums[me, KV_ROW] = jnp.sum(jnp.where(diagonal, row_sums, 0.0), axis=0, keepdims=True)
-    own_norm = norm_a[...] + norm_b[...]
+    own_norm = norm_v[0] + norm_v[1]
     sums[me, NORM_ROW] = jnp.concatenate([own_norm, own_norm], axis=1)
     send_sums(1, SUM_ROWS - 1, 1)
 
@@ -303,19 +305,19 @@
     gathered = pl.pallas_call(
         gather_kernel,
         out_shape=tuple(pltpu.VMEM(shape, dtype) for shape, dtype in held),
-        in_specs=[any_spec] * 6 + [vmem_spec] * 2,
+        in_specs=[any_spec] * 8,
         out_specs=tuple(vmem_spec for _ in held),
         scratch_shapes=[
             pltpu.VMEM((ROWS, COLS), f32),
             pltpu.VMEM((ROWS, COLS), f32),
             pltpu.VMEM((KV, ROWS), f32),
             pltpu.VMEM((KV, ROWS), f32),
-            pltpu.VMEM((1, COLS), f32),
+            pltpu.VMEM((2, 1, 64), f32),
             pltpu.VMEM((8, SUM_ROWS, 1, LANES), f32),
             pltpu.VMEM((4, 8, LANES), f32),
             pltpu.VMEM((4, 2, 8, LANES), f32),
             pltpu.VMEM((64, LANES), f32),
-            dma((2 * TILES + 4,)),
+            dma((2 * TILES + 6,)),
             dma((2, 8)),
             dma((2, 8)),
             dma((3, units)),
@@ -332,8 +334,13 @@
         ),
         name="gather",
     )(
-        weight_query, smooth_query, weight_key.T, smooth_key.T, weight_value.T, smooth_value.T,
-        norm_train.reshape(1, 64), norm_step.reshape(1, 64),
+        *(
+            pltpu.with_memory_space_constraint(a, pltpu.HBM)
+            for a in (
+                weight_query, smooth_query, weight_key.T, smooth_key.T, weight_value.T, smooth_value.T,
+                norm_train.reshape(1, 64), norm_step.reshape(1, 64),
+            )
+        )
     )
     outs = (
         ((D_MODEL, COLS), bf16),

time: 67.4 us -> 58 us (0.86)
  local copies, waits for them, and re-layouts: 8.1 us -> 0 us
  Pallas kernels: 58.4 us -> 57.3 us
    unnamed x16 -> x0, local copies, waits for them, and re-layouts: 8.1 us -> none
    pallas_call x1, Pallas kernels: 53.9 us -> 52.8 us  [on_device(): pl.pallas_call(gather_kernel, out_shape=tuple((pltpu.VMEM(shape, dtype) f...]
where the time goes in v2:
time: 58 us; the launch traced here: 57.9 us
  Pallas kernels  57.3 us (99%)
  between operations  0.65 us (1%)
    pallas_call x1, Pallas kernels, on_device(): pl.pallas_call(gather_kernel, out_shape=tuple((pltpu.VMEM(shape, dtype) f...  52.8 us
    pallas_call x1, Pallas kernels, on_device(): pl.pallas_call(write_kernel, out_shape=tuple((jax.ShapeDtypeStruct(shape,...  4.45 us

profile of v2, /device:TPU:1, one launch (start us, length us, event | category | flops | bytes accessed | tf_op | source)
XLA Modules:
  0.0 57.9 jit_solution(13034087802191614006)
XLA Ops:
  0.6 52.8 %gather.1 = (bf16[8192,512]{1,0:T(8,128)(2,1)S(1)}, bf16[64,8192]{1,0:T(8,128)(2,1)S(1)}, f32[1024,512]{1,0:T(8,128)S(1)}, f32[64,1024]{1,0:T(8,128)S(1)}, f32[1...) custom-call(f32[1024,512]{1,0:T(8,128)} %wq.1, f32[1024,512]{1,0:T(8,128)} %sq.1, ...), custom_call_target="tpu_custom_call" | custom-call | tf_op jit(solution)/shard_map/gather/pallas_call | solution.py:305
  53.5 4.4 %write.1 = (bf16[8192,512]{1,0:T(8,128)(2,1)}, bf16[32,8192]{1,0:T(8,128)(2,1)}, bf16[32,8192]{1,0:T(8,128)(2,1)}, f32[1,512]{1,0:T(1,128)}, f32[1,32]{1,0:T(1,1...) custom-call(bf16[8192,512]{1,0:T(8,128)(2,1)S(1)} %get-tuple-element, ...), custom_call_target="tpu_custom_call" | custom-call | tf_op jit(solution)/shard_map/write/pallas_call | solution.py:357

commit v3 on v2

--- a/solution.py
+++ b/solution.py
@@ -35,47 +35,59 @@
     wq, sq, wk, sk, wv, sv, norm_a, norm_b,
     out_q, out_kv, res_q, res_kv, fac_q, fac_k, fac_v, norm_out,
     wq_v, sq_v, wkv_v, skv_v, norm_v, sums, norm_y, norm_z, norm_all,
-    in_sem, sum_send, sum_recv, own_send, fwd_send, rel_send,
-    side_recv, far_recv, rel_recv, norm_send, norm_recv,
+    in_sem, send_sem, sum_send, sum_recv, side_recv, far_recv, rel_recv, norm_send, norm_recv, go,
 ):
     x, c = lax.axis_index("zero_0"), lax.axis_index("zero_1")
     z, y = lax.axis_index("width_0"), lax.axis_index("width_1")
     me = x * 2 + c
     right, left = lax.rem(x + 1, 4), lax.rem(x + 3, 4)
-    sides = ((left, right), (right, left))
-
-    loads = []
-
-    def load(src, dst):
-        copy = pltpu.make_async_copy(src, dst, in_sem.at[len(loads)])
-        copy.start()
-        loads.append(copy)
+    partner = {"zero_1": 1 - c}
+
+    def load(src, dst, which):
+        pltpu.make_async_copy(src, dst, in_sem.at[which]).start()
+
+    def wait_bytes(ref, sem):
+        pltpu.make_async_copy(ref, ref, sem).wait()
 
     for t in range(TILES):
         cols = pl.ds(t * LANES, LANES)
-        load(wq.at[:, cols], wq_v.at[:, cols])
-        load(sq.at[:, cols], sq_v.at[:, cols])
-    load(wk, wkv_v.at[pl.ds(0, 32), :])
-    load(sk, skv_v.at[pl.ds(0, 32), :])
-    load(wv, wkv_v.at[pl.ds(32, 32), :])
-    load(sv, skv_v.at[pl.ds(32, 32), :])
-    load(norm_a, norm_v.at[0])
-    load(norm_b, norm_v.at[1])
+        load(wq.at[:, cols], wq_v.at[:, cols], t)
+        load(sq.at[:, cols], sq_v.at[:, cols], t)
+    load(wk, wkv_v.at[pl.ds(0, 32), :], KV_ROW)
+    load(sk, skv_v.at[pl.ds(0, 32), :], KV_ROW)
+    load(wv, wkv_v.at[pl.ds(32, 32), :], KV_ROW)
+    load(sv, skv_v.at[pl.ds(32, 32), :], KV_ROW)
+    load(norm_a, norm_v.at[0], NORM_ROW)
+    load(norm_b, norm_v.at[1], NORM_ROW)
 
     def group_peer(d):
         other = lax.rem(me + d, 8)
         return {"zero_0": other // 2, "zero_1": lax.rem(other, 2)}
 
     barrier = pltpu.get_barrier_semaphore()
-    for d in (4, 5, 3, 2, 6, 7, 1):
-        pl.semaphore_signal(barrier, inc=1, device_id=group_peer(d), device_id_type=MESH)
     for d in (2, 1, 3):
-        pl.semaphore_signal(barrier, inc=1, device_id={"width_1": lax.rem(y + d, 4)}, device_id_type=MESH)
-        pl.semaphore_signal(barrier, inc=1, device_id={"width_0": lax.rem(z + d, 4)}, device_id_type=MESH)
+        device = {"zero_0": lax.rem(x + d, 4), "zero_1": 1}
+        pl.semaphore_signal(barrier, inc=1, device_id=device, device_id_type=MESH)
+
+    @pl.when(c == 0)
+    def _():
+        pl.semaphore_signal(barrier, inc=1, device_id=partner, device_id_type=MESH)
+        for d in (2, 1, 3):
+            pl.semaphore_signal(barrier, inc=1, device_id={"width_1": lax.rem(y + d, 4)}, device_id_type=MESH)
+            pl.semaphore_signal(barrier, inc=1, device_id={"width_0": lax.rem(z + d, 4)}, device_id_type=MESH)
+
+    def wait_for_group():
+        @pl.when(c == 1)
+        def _():
+            pl.semaphore_wait(barrier, 7)
+            pl.semaphore_signal(go, inc=1, device_id=partner, device_id_type=MESH)
+
+        @pl.when(c == 0)
+        def _():
+            pl.semaphore_wait(go, 1)
 
     def sum_tile(t):
-        loads[2 * t].wait()
-        loads[2 * t + 1].wait()
+        wait_bytes(wq_v.at[:, pl.ds(0, 2 * LANES)], in_sem.at[t])
         cols = pl.ds(t * LANES, LANES)
 
         def body(i, acc):
@@ -92,33 +104,21 @@
             pltpu.make_async_remote_copy(
                 src_ref=sums.at[me, pl.ds(first, count)],
                 dst_ref=sums.at[me, pl.ds(first, count)],
-                send_sem=sum_send.at[which, d],
-                recv_sem=sum_recv.at[which, d],
+                send_sem=sum_send,
+                recv_sem=sum_recv.at[which],
                 device_id=group_peer(d),
                 device_id_type=MESH,
             ).start()
 
-    def sums_copy(first, count, which, d):
-        other = lax.rem(me + 8 - d, 8)
-        return pltpu.make_async_remote_copy(
-            src_ref=sums.at[other, pl.ds(first, count)],
-            dst_ref=sums.at[other, pl.ds(first, count)],
-            send_sem=sum_send.at[which, d],
-            recv_sem=sum_recv.at[which, d],
-            device_id=group_peer(d),
-            device_id_type=MESH,
-        )
-
     lane_of = lax.broadcasted_iota(jnp.int32, (KV, LANES), 1)
     diagonal = lane_of == lax.broadcasted_iota(jnp.int32, (KV, LANES), 0)
 
     sum_tile(0)
-    pl.semaphore_wait(barrier, 13)
+    wait_for_group()
     send_sums(0, 1, 0)
     for t in range(1, TILES):
         sum_tile(t)
-    for copy in loads[2 * TILES :]:
-        copy.wait()
+    wait_bytes(wq_v.at[pl.ds(0, 4 * 32 * ROWS // COLS), :], in_sem.at[KV_ROW])
     acc = jnp.zeros((KV, LANES), jnp.float32)
     for j in range(ROWS // LANES):
         cols = pl.ds(j * LANES, LANES)
@@ -127,6 +127,7 @@
         acc = acc + jnp.abs(r)
     row_sums = jnp.sum(acc, axis=1, keepdims=True)
     sums[me, KV_ROW] = jnp.sum(jnp.where(diagonal, row_sums, 0.0), axis=0, keepdims=True)
+    wait_bytes(norm_v, in_sem.at[NORM_ROW])
     own_norm = norm_v[0] + norm_v[1]
     sums[me, NORM_ROW] = jnp.concatenate([own_norm, own_norm], axis=1)
     send_sums(1, SUM_ROWS - 1, 1)
@@ -138,25 +139,19 @@
             return out_q.at[rows, pl.ds(tile * LANES, LANES)]
         return out_kv.at[:, pl.ds(pl.multiple_of(origin * ROWS + half * HALF, HALF), HALF)]
 
-    def unit_copy(origin, k, send_sem, recv_sem, device):
+    def unit_copy(origin, k, recv_sem, device):
         ref = place(origin, k)
         return pltpu.make_async_remote_copy(
             src_ref=ref, dst_ref=ref, send_sem=send_sem, recv_sem=recv_sem, device_id=device, device_id_type=MESH
         )
 
-    partner = {"zero_1": 1 - c}
     to_right, to_left = {"zero_0": right}, {"zero_0": left}
-    sends = []
-
-    def send(copy):
-        copy.start()
-        sends.append(copy)
 
     def send_own(k):
         ways = [(0, to_right), (1, to_left)]
         for side, device in ways if UNITS[k][1] == 0 else ways[::-1]:
-            send(unit_copy(me, k, own_send.at[side, k], side_recv.at[side, k], device))
-        send(unit_copy(me, k, own_send.at[2, k], rel_recv.at[0, k], partner))
+            unit_copy(me, k, side_recv.at[side, k], device).start()
+        unit_copy(me, k, rel_recv, partner).start()
 
     def narrow_tile(t):
         total = sums[0, t]
@@ -190,74 +185,71 @@
                     out_kv[:, there] = (res_kv[:, pl.ds(at, LANES)] * scale).astype(jnp.bfloat16)
             send_own(2 * t + half)
 
-    for d in range(1, 8):
-        sums_copy(0, 1, 0, d).wait_recv()
+    wait_bytes(sums.at[pl.ds(0, 7), pl.ds(0, 1)], sum_recv.at[0])
     narrow_tile(0)
-    for d in range(1, 8):
-        sums_copy(1, SUM_ROWS - 1, 1, d).wait_recv()
+    wait_bytes(sums.at[pl.ds(0, 7), pl.ds(1, SUM_ROWS - 1)], sum_recv.at[1])
     for t in range(1, TILES + 1):
         narrow_tile(t)
 
-    def norm_copy(buf, at, stage, d, axis, here):
+    def norm_copy(buf, at, stage, device):
         return pltpu.make_async_remote_copy(
             src_ref=buf.at[at],
             dst_ref=buf.at[at],
-            send_sem=norm_send.at[stage, d],
-            recv_sem=norm_recv.at[stage, d],
-            device_id={axis: lax.rem(here + d, 4)},
+            send_sem=norm_send.at[stage],
+            recv_sem=norm_recv.at[stage],
+            device_id=device,
             device_id_type=MESH,
         )
 
-    for other in range(8):
-        norm_y[y, pl.ds(other, 1), :] = sums[other, NORM_ROW]
-    for d in (2, 1, 3):
-        norm_copy(norm_y, y, 0, d, "width_1", y).start()
+    def norm_along_y():
+        pl.semaphore_wait(barrier, 6)
+        for other in range(8):
+            norm_y[y, pl.ds(other, 1), :] = sums[other, NORM_ROW]
+        for d in (2, 1, 3):
+            norm_copy(norm_y, y, 0, {"width_1": lax.rem(y + d, 4)}).start()
 
     def norm_along_z():
-        for d in (1, 3, 2):
-            norm_copy(norm_y, lax.rem(y + 4 - d, 4), 0, d, "width_1", y).wait_recv()
+        wait_bytes(norm_y.at[pl.ds(0, 3)], norm_recv.at[0])
         low = lax.broadcasted_iota(jnp.int32, (8, LANES), 1) < 64
         norm_z[z, 0] = jnp.where(low, norm_y[0], norm_y[1])
         norm_z[z, 1] = jnp.where(low, norm_y[2], norm_y[3])
         for d in (2, 1, 3):
-            norm_copy(norm_z, z, 1, d, "width_0", z).start()
+            norm_copy(norm_z, z, 1, {"width_0": lax.rem(z + d, 4)}).start()
 
     def norm_end():
-        for d in (1, 3, 2):
-            norm_copy(norm_z, lax.rem(z + 4 - d, 4), 1, d, "width_0", z).wait_recv()
+        wait_bytes(norm_z.at[pl.ds(0, 3)], norm_recv.at[1])
         for zz in range(4):
             for pair in range(2):
                 for other in range(8):
                     norm_all[pl.ds(other * 8 + zz * 2 + pair, 1), :] = norm_z[zz, pair, pl.ds(other, 1), :]
         norm_out[...] = norm_all[...].astype(jnp.bfloat16)
-        for d in range(1, 4):
-            norm_copy(norm_y, y, 0, d, "width_1", y).wait_send()
-            norm_copy(norm_z, z, 1, d, "width_0", z).wait_send()
+        wait_bytes(norm_y.at[pl.ds(0, 3)], norm_send.at[0])
+        wait_bytes(norm_z.at[pl.ds(0, 3)], norm_send.at[1])
+
+    def norm_to_partner():
+        return norm_copy(norm_out, pl.ds(0, 64), 2, partner)
 
     far = lax.rem(x + 2, 4)
+    norm_steps = {1: norm_along_y, 3: norm_along_z, 5: norm_end, 6: lambda: norm_to_partner().start()}
     for k in range(len(UNITS)):
         for side in range(2):
             origin = (left if side == 0 else right) * 2 + c
-            unit_copy(origin, k, own_send.at[side, k], side_recv.at[side, k], to_right).wait_recv()
+            unit_copy(origin, k, side_recv.at[side, k], to_right).wait_recv()
             if UNITS[k][1] == side:
-                send(unit_copy(origin, k, fwd_send.at[k], far_recv.at[k], to_right if side == 0 else to_left))
-            send(unit_copy(origin, k, rel_send.at[side, k], rel_recv.at[1 + side, k], partner))
-        if k == 2:
-            norm_along_z()
-        if k == 4:
-            norm_end()
+                unit_copy(origin, k, far_recv.at[k], to_right if side == 0 else to_left).start()
+            unit_copy(origin, k, rel_recv, partner).start()
+        if k in norm_steps:
+            pl.when(c == 0)(norm_steps[k])
+    pl.when(c == 0)(lambda: norm_to_partner().wait_send())
+    pl.when(c == 1)(lambda: norm_to_partner().wait_recv())
     for k in range(len(UNITS)):
-        unit_copy(far * 2 + c, k, fwd_send.at[k], far_recv.at[k], to_right).wait_recv()
-        send(unit_copy(far * 2 + c, k, rel_send.at[2, k], rel_recv.at[3, k], partner))
-
-    for d in range(1, 8):
-        sums_copy(0, 1, 0, d).wait_send()
-        sums_copy(1, SUM_ROWS - 1, 1, d).wait_send()
-    for copy in sends:
-        copy.wait_send()
-    for which, origin in enumerate((x, left, right, far)):
-        for k in range(len(UNITS)):
-            unit_copy(origin * 2 + 1 - c, k, own_send.at[2, k], rel_recv.at[which, k], partner).wait_recv()
+        unit_copy(far * 2 + c, k, far_recv.at[k], to_right).wait_recv()
+        unit_copy(far * 2 + c, k, rel_recv, partner).start()
+
+    shard_rows = ROWS + KV * ROWS // COLS
+    wait_bytes(sums.at[pl.ds(0, 7)], sum_send)
+    wait_bytes(out_q.at[pl.ds(0, 7 * shard_rows), :], send_sem)
+    wait_bytes(out_q.at[pl.ds(0, 4 * shard_rows), :], rel_recv)
 
 
 def write_kernel(
@@ -317,17 +309,16 @@
             pltpu.VMEM((4, 8, LANES), f32),
             pltpu.VMEM((4, 2, 8, LANES), f32),
             pltpu.VMEM((64, LANES), f32),
-            dma((2 * TILES + 6,)),
-            dma((2, 8)),
-            dma((2, 8)),
-            dma((3, units)),
-            dma((units,)),
-            dma((3, units)),
+            dma((SUM_ROWS,)),
+            dma,
+            dma,
+            dma((2,)),
             dma((2, units)),
             dma((units,)),
-            dma((4, units)),
-            dma((2, 4)),
-            dma((2, 4)),
+            dma,
+            dma((3,)),
+            dma((3,)),
+            pltpu.SemaphoreType.REGULAR,
         ],
         compiler_params=pltpu.CompilerParams(
             collective_id=0, has_side_effects=True, vmem_limit_bytes=16 * 1024 * 1024

time: 58 us -> 55 us (0.948)
  Pallas kernels: 57.3 us -> 54.2 us
    pallas_call x1, Pallas kernels: 52.8 us -> 49.8 us  [on_device(): pl.pallas_call(gather_kernel, out_shape=tuple((pltpu.VMEM(shape, dtype) f...]
where the time goes in v3:
time: 55 us; the launch traced here: 54.9 us
  Pallas kernels  54.2 us (99%)
  between operations  0.65 us (1%)
    pallas_call x1, Pallas kernels, on_device(): pl.pallas_call(gather_kernel, out_shape=tuple((pltpu.VMEM(shape, dtype) f...  49.8 us
    pallas_call x1, Pallas kernels, on_device(): pl.pallas_call(write_kernel, out_shape=tuple((jax.ShapeDtypeStruct(shape,...  4.45 us

profile of v3, /device:TPU:1, one launch (start us, length us, event | category | flops | bytes accessed | tf_op | source)
XLA Modules:
  0.0 54.9 jit_solution(10037949712918977166)
XLA Ops:
  0.6 49.8 %gather.1 = (bf16[8192,512]{1,0:T(8,128)(2,1)S(1)}, bf16[64,8192]{1,0:T(8,128)(2,1)S(1)}, f32[1024,512]{1,0:T(8,128)S(1)}, f32[64,1024]{1,0:T(8,128)S(1)}, f32[1...) custom-call(f32[1024,512]{1,0:T(8,128)} %wq.1, f32[1024,512]{1,0:T(8,128)} %sq.1, ...), custom_call_target="tpu_custom_call" | custom-call | tf_op jit(solution)/shard_map/gather/pallas_call | solution.py:297
  50.4 4.4 %write.1 = (bf16[8192,512]{1,0:T(8,128)(2,1)}, bf16[32,8192]{1,0:T(8,128)(2,1)}, bf16[32,8192]{1,0:T(8,128)(2,1)}, f32[1,512]{1,0:T(1,128)}, f32[1,32]{1,0:T(1,1...) custom-call(bf16[8192,512]{1,0:T(8,128)(2,1)S(1)} %get-tuple-element, ...), custom_call_target="tpu_custom_call" | custom-call | tf_op jit(solution)/shard_map/write/pallas_call | solution.py:348

commit v4 on v3

--- a/solution.py
+++ b/solution.py
@@ -21,20 +21,42 @@
 LANES = 128
 TILES = COLS // LANES
 STEP = 128
-KV_ROW, NORM_ROW = TILES, TILES + 1
-SUM_ROWS = TILES + 2
-
-UNITS = tuple((tile, half) for tile in range(TILES + 1) for half in range(2))
+KV_ROW, NORM_ROW, MAX_ROW = TILES, TILES + 1, TILES + 2
+SUM_ROWS = TILES + 3
+
+FIRST = 192
+CODED = ((0, 0, FIRST, 0), (0, FIRST, HALF - FIRST, 0), (0, HALF, FIRST, 1), (0, HALF + FIRST, HALF - FIRST, 1))
+UNITS = CODED + tuple((tile, half * HALF, HALF, half) for tile in range(1, TILES + 1) for half in range(2))
+ORDER = (
+    (0, 1, 2, 3, *range(4, len(UNITS))),
+    (2, 3, 0, 1, *range(4, len(UNITS))),
+)
+CODE = 180.0
 
 
 def mix(smooth, weight):
     return keep_rate * smooth + (1.0 - keep_rate) * weight
+
+
+def encode(x, scale):
+    v = x * scale
+    for _ in range(4):
+        v = v * v
+    return jnp.where(x < 0, -v, v).astype(jnp.bfloat16)
+
+
+def decode(code):
+    v = code.astype(jnp.float32)
+    root = jnp.abs(v)
+    for _ in range(4):
+        root = lax.rsqrt(root)
+    return jnp.where(v < 0, -root, root)
 
 
 def gather_kernel(
     wq, sq, wk, sk, wv, sv, norm_a, norm_b,
     out_q, out_kv, res_q, res_kv, fac_q, fac_k, fac_v, norm_out,
-    wq_v, sq_v, wkv_v, skv_v, norm_v, sums, norm_y, norm_z, norm_all,
+    wq_v, sq_v, wkv_v, skv_v, norm_v, coded, sums, norm_y, norm_z, norm_all,
     in_sem, send_sem, sum_send, sum_recv, side_recv, far_recv, rel_recv, norm_send, norm_recv, go,
 ):
     x, c = lax.axis_index("zero_0"), lax.axis_index("zero_1")
@@ -90,32 +112,90 @@
         wait_bytes(wq_v.at[:, pl.ds(0, 2 * LANES)], in_sem.at[t])
         cols = pl.ds(t * LANES, LANES)
 
-        def body(i, acc):
+        def body(i, carry):
+            acc, top = carry
             rows = pl.ds(pl.multiple_of(i * STEP, STEP), STEP)
             r = mix(sq_v[rows, cols], wq_v[rows, cols])
             res_q[rows, cols] = r
-            return acc + jnp.sum(jnp.abs(r).reshape(STEP // 8, 8, LANES), axis=0)
-
-        acc = lax.fori_loop(0, ROWS // STEP, body, jnp.zeros((8, LANES), jnp.float32))
+            size = jnp.abs(r).reshape(STEP // 8, 8, LANES)
+            acc = acc + jnp.sum(size, axis=0)
+            return acc, jnp.maximum(top, jnp.max(size, axis=0)) if t == 0 else top
+
+        none = jnp.zeros((8, LANES), jnp.float32)
+        acc, top = lax.fori_loop(0, ROWS // STEP, body, (none, none))
         sums[me, t] = jnp.sum(acc, axis=0, keepdims=True)
-
-    def send_sums(first, count, which):
+        return jnp.max(top, axis=0, keepdims=True)
+
+    def send_sums():
         for d in (4, 5, 3, 2, 6, 7, 1):
             pltpu.make_async_remote_copy(
-                src_ref=sums.at[me, pl.ds(first, count)],
-                dst_ref=sums.at[me, pl.ds(first, count)],
+                src_ref=sums.at[me],
+                dst_ref=sums.at[me],
                 send_sem=sum_send,
-                recv_sem=sum_recv.at[which],
+                recv_sem=sum_recv,
                 device_id=group_peer(d),
                 device_id_type=MESH,
             ).start()
 
+    def final_place(origin, k):
+        tile, row, rows, _ = UNITS[k]
+        if tile < TILES:
+            return out_q.at[pl.ds(pl.multiple_of((origin * 2 + c) * ROWS + row, 64), rows), pl.ds(tile * LANES, LANES)]
+        return out_kv.at[:, pl.ds(pl.multiple_of((origin * 2 + c) * ROWS + row, HALF), rows)]
+
+    def place(origin, k):
+        _, row, rows, _ = UNITS[k]
+        return coded.at[origin, pl.ds(row, rows)] if k < len(CODED) else final_place(origin, k)
+
+    def unit_copy(ref, recv_sem, device):
+        return pltpu.make_async_remote_copy(
+            src_ref=ref, dst_ref=ref, send_sem=send_sem, recv_sem=recv_sem, device_id=device, device_id_type=MESH
+        )
+
+    to_right, to_left = {"zero_0": right}, {"zero_0": left}
+
+    def send_right(k):
+        unit_copy(place(x, k), side_recv.at[0, k], to_right).start()
+
+    def send_left(k):
+        unit_copy(place(x, k), side_recv.at[1, k], to_left).start()
+
+    def relay(origin, k):
+        unit_copy(final_place(origin, k), rel_recv, partner).start()
+
+    def encode_rows(k, scale):
+        _, row, rows, _ = UNITS[k]
+
+        def body(i, carry):
+            at = pl.ds(pl.multiple_of(row + i * 64, 64), 64)
+            coded[x, at, :] = encode(res_q[at, 0:LANES], scale)
+            return carry
+
+        lax.fori_loop(0, rows // 64, body, 0)
+
+    def decode_rows(origin, k, scale):
+        _, row, rows, _ = UNITS[k]
+        own = sums[origin * 2 + c, MAX_ROW] * scale
+
+        def body(i, carry):
+            at = pl.multiple_of(row + i * 64, 64)
+            there = pl.ds(pl.multiple_of((origin * 2 + c) * ROWS + at, 64), 64)
+            out_q[there, 0:LANES] = (decode(coded[origin, pl.ds(at, 64), :]) * own).astype(jnp.bfloat16)
+            return carry
+
+        lax.fori_loop(0, rows // 64, body, 0)
+
     lane_of = lax.broadcasted_iota(jnp.int32, (KV, LANES), 1)
     diagonal = lane_of == lax.broadcasted_iota(jnp.int32, (KV, LANES), 0)
 
-    sum_tile(0)
+    top = jnp.maximum(sum_tile(0), 1e-30)
+    sums[me, MAX_ROW] = top
+    scale = CODE / top
+    encode_rows(0, scale)
+    encode_rows(2, scale)
     wait_for_group()
-    send_sums(0, 1, 0)
+    send_right(0)
+    send_left(2)
     for t in range(1, TILES):
         sum_tile(t)
     wait_bytes(wq_v.at[pl.ds(0, 4 * 32 * ROWS // COLS), :], in_sem.at[KV_ROW])
@@ -130,34 +210,23 @@
     wait_bytes(norm_v, in_sem.at[NORM_ROW])
     own_norm = norm_v[0] + norm_v[1]
     sums[me, NORM_ROW] = jnp.concatenate([own_norm, own_norm], axis=1)
-    send_sums(1, SUM_ROWS - 1, 1)
-
-    def place(origin, k):
-        tile, half = UNITS[k]
-        if tile < TILES:
-            rows = pl.ds(pl.multiple_of(origin * ROWS + half * HALF, HALF), HALF)
-            return out_q.at[rows, pl.ds(tile * LANES, LANES)]
-        return out_kv.at[:, pl.ds(pl.multiple_of(origin * ROWS + half * HALF, HALF), HALF)]
-
-    def unit_copy(origin, k, recv_sem, device):
-        ref = place(origin, k)
-        return pltpu.make_async_remote_copy(
-            src_ref=ref, dst_ref=ref, send_sem=send_sem, recv_sem=recv_sem, device_id=device, device_id_type=MESH
-        )
-
-    to_right, to_left = {"zero_0": right}, {"zero_0": left}
-
-    def send_own(k):
-        ways = [(0, to_right), (1, to_left)]
-        for side, device in ways if UNITS[k][1] == 0 else ways[::-1]:
-            unit_copy(me, k, side_recv.at[side, k], device).start()
-        unit_copy(me, k, rel_recv, partner).start()
-
-    def narrow_tile(t):
+    send_sums()
+    encode_rows(1, scale)
+    send_right(1)
+    encode_rows(3, scale)
+    for k in (3, 0, 1):
+        send_left(k)
+    for k in (2, 3):
+        send_right(k)
+
+    def factor_of(t):
         total = sums[0, t]
         for other in range(1, 8):
             total = total + sums[other, t]
-        factor = total * (1.0 / D_MODEL)
+        return total * (1.0 / D_MODEL)
+
+    def narrow_tile(t):
+        factor = factor_of(t)
         if t < TILES:
             fac_q[:, pl.ds(t * LANES, LANES)] = factor
             scale = 1.0 / factor
@@ -183,13 +252,20 @@
                     at = half * HALF + j * LANES
                     there = pl.ds(pl.multiple_of(me * ROWS + at, LANES), LANES)
                     out_kv[:, there] = (res_kv[:, pl.ds(at, LANES)] * scale).astype(jnp.bfloat16)
-            send_own(2 * t + half)
-
-    wait_bytes(sums.at[pl.ds(0, 7), pl.ds(0, 1)], sum_recv.at[0])
-    narrow_tile(0)
-    wait_bytes(sums.at[pl.ds(0, 7), pl.ds(1, SUM_ROWS - 1)], sum_recv.at[1])
+            k = len(CODED) + 2 * (t - 1) + half
+            for go_there in (send_right, send_left) if half == 0 else (send_left, send_right):
+                go_there(k)
+            relay(x, k)
+
+    wait_bytes(sums.at[pl.ds(0, 7)], sum_recv)
     for t in range(1, TILES + 1):
         narrow_tile(t)
+    first_factor = factor_of(0)
+    fac_q[:, 0:LANES] = first_factor
+    first_scale = 1.0 / (CODE * first_factor)
+    for k in range(len(CODED)):
+        decode_rows(x, k, first_scale)
+        relay(x, k)
 
     def norm_copy(buf, at, stage, device):
         return pltpu.make_async_remote_copy(
@@ -230,21 +306,27 @@
         return norm_copy(norm_out, pl.ds(0, 64), 2, partner)
 
     far = lax.rem(x + 2, 4)
-    norm_steps = {1: norm_along_y, 3: norm_along_z, 5: norm_end, 6: lambda: norm_to_partner().start()}
-    for k in range(len(UNITS)):
+    norm_steps = {2: norm_along_y, 4: norm_along_z, 6: norm_end, 7: lambda: norm_to_partner().start()}
+
+    def hand_on(origin, k):
+        if k < len(CODED):
+            decode_rows(origin, k, first_scale)
+        relay(origin, k)
+
+    for i in range(len(UNITS)):
         for side in range(2):
-            origin = (left if side == 0 else right) * 2 + c
-            unit_copy(origin, k, side_recv.at[side, k], to_right).wait_recv()
-            if UNITS[k][1] == side:
-                unit_copy(origin, k, far_recv.at[k], to_right if side == 0 else to_left).start()
-            unit_copy(origin, k, rel_recv, partner).start()
-        if k in norm_steps:
-            pl.when(c == 0)(norm_steps[k])
+            k, origin = ORDER[side][i], left if side == 0 else right
+            unit_copy(place(origin, k), side_recv.at[side, k], partner).wait_recv()
+            if UNITS[k][3] == side:
+                unit_copy(place(origin, k), far_recv.at[k], to_right if side == 0 else to_left).start()
+            hand_on(origin, k)
+        if i in norm_steps:
+            pl.when(c == 0)(norm_steps[i])
     pl.when(c == 0)(lambda: norm_to_partner().wait_send())
     pl.when(c == 1)(lambda: norm_to_partner().wait_recv())
-    for k in range(len(UNITS)):
-        unit_copy(far * 2 + c, k, far_recv.at[k], to_right).wait_recv()
-        unit_copy(far * 2 + c, k, rel_recv, partner).start()
+    for k in (0, 2, 1, 3, *range(len(CODED), len(UNITS))):
+        unit_copy(place(far, k), far_recv.at[k], partner).wait_recv()
+        hand_on(far, k)
 
     shard_rows = ROWS + KV * ROWS // COLS
     wait_bytes(sums.at[pl.ds(0, 7)], sum_send)
@@ -305,6 +387,7 @@
             pltpu.VMEM((KV, ROWS), f32),
             pltpu.VMEM((KV, ROWS), f32),
             pltpu.VMEM((2, 1, 64), f32),
+            pltpu.VMEM((4, ROWS, LANES), bf16),
             pltpu.VMEM((8, SUM_ROWS, 1, LANES), f32),
             pltpu.VMEM((4, 8, LANES), f32),
             pltpu.VMEM((4, 2, 8, LANES), f32),
@@ -312,7 +395,7 @@
             dma((SUM_ROWS,)),
             dma,
             dma,
-            dma((2,)),
+            dma,
             dma((2, units)),
             dma((units,)),
             dma,

time: 55 us -> 51.7 us (0.940)
  Pallas kernels: 54.2 us -> 50.9 us
    pallas_call x1, Pallas kernels: 49.8 us -> 46.4 us  [on_device(): pl.pallas_call(gather_kernel, out_shape=tuple((pltpu.VMEM(shape, dtype) f...]
where the time goes in v4:
time: 51.7 us; the launch traced here: 51.5 us
  Pallas kernels  50.9 us (98%)
  between operations  0.65 us (1%)
    pallas_call x1, Pallas kernels, on_device(): pl.pallas_call(gather_kernel, out_shape=tuple((pltpu.VMEM(shape, dtype) f...  46.4 us
    pallas_call x1, Pallas kernels, on_device(): pl.pallas_call(write_kernel, out_shape=tuple((jax.ShapeDtypeStruct(shape,...  4.45 us

profile of v4, /device:TPU:1, one launch (start us, length us, event | category | flops | bytes accessed | tf_op | source)
XLA Modules:
  0.0 51.5 jit_solution(14405157669523354433)
XLA Ops:
  0.6 46.4 %gather.1 = (bf16[8192,512]{1,0:T(8,128)(2,1)S(1)}, bf16[64,8192]{1,0:T(8,128)(2,1)S(1)}, f32[1024,512]{1,0:T(8,128)S(1)}, f32[64,1024]{1,0:T(8,128)S(1)}, f32[1...) custom-call(f32[1024,512]{1,0:T(8,128)} %wq.1, f32[1024,512]{1,0:T(8,128)} %sq.1, ...), custom_call_target="tpu_custom_call" | custom-call | tf_op jit(solution)/shard_map/gather/pallas_call | solution.py:379
  47.1 4.4 %write.1 = (bf16[8192,512]{1,0:T(8,128)(2,1)}, bf16[32,8192]{1,0:T(8,128)(2,1)}, bf16[32,8192]{1,0:T(8,128)(2,1)}, f32[1,512]{1,0:T(1,128)}, f32[1,32]{1,0:T(1,1...) custom-call(bf16[8192,512]{1,0:T(8,128)(2,1)S(1)} %get-tuple-element, ...), custom_call_target="tpu_custom_call" | custom-call | tf_op jit(solution)/shard_map/write/pallas_call | solution.py:431

commit v5 on v4

--- a/solution.py
+++ b/solution.py
@@ -22,14 +22,15 @@
 TILES = COLS // LANES
 STEP = 128
 KV_ROW, NORM_ROW, MAX_ROW = TILES, TILES + 1, TILES + 2
-SUM_ROWS = TILES + 3
+SUM_ROWS = TILES + 4
 
 FIRST = 192
-CODED = ((0, 0, FIRST, 0), (0, FIRST, HALF - FIRST, 0), (0, HALF, FIRST, 1), (0, HALF + FIRST, HALF - FIRST, 1))
+PIECES = ((0, FIRST), (192, 128), (320, 192))
+CODED = tuple((0, half * HALF + row, rows, half) for half in range(2) for row, rows in PIECES)
 UNITS = CODED + tuple((tile, half * HALF, HALF, half) for tile in range(1, TILES + 1) for half in range(2))
 ORDER = (
-    (0, 1, 2, 3, *range(4, len(UNITS))),
-    (2, 3, 0, 1, *range(4, len(UNITS))),
+    (0, 1, 2, 3, 4, 5, *range(6, len(UNITS))),
+    (3, 4, 5, 0, 1, 2, *range(6, len(UNITS))),
 )
 CODE = 180.0
 
@@ -57,7 +58,7 @@
     wq, sq, wk, sk, wv, sv, norm_a, norm_b,
     out_q, out_kv, res_q, res_kv, fac_q, fac_k, fac_v, norm_out,
     wq_v, sq_v, wkv_v, skv_v, norm_v, coded, sums, norm_y, norm_z, norm_all,
-    in_sem, send_sem, sum_send, sum_recv, side_recv, far_recv, rel_recv, norm_send, norm_recv, go,
+    in_sem, send_sem, sum_send, sum_recv, side_recv, far_recv, rel_recv, norm_send, norm_recv, go, vouch,
 ):
     x, c = lax.axis_index("zero_0"), lax.axis_index("zero_1")
     z, y = lax.axis_index("width_0"), lax.axis_index("width_1")
@@ -68,63 +69,98 @@
     def load(src, dst, which):
         pltpu.make_async_copy(src, dst, in_sem.at[which]).start()
 
+    def load_rows(t, first, rows, which):
+        at = (pl.ds(first, rows), pl.ds(t * LANES, LANES))
+        load(wq.at[at], wq_v.at[at], which)
+        load(sq.at[at], sq_v.at[at], which)
+
     def wait_bytes(ref, sem):
         pltpu.make_async_copy(ref, ref, sem).wait()
 
-    for t in range(TILES):
-        cols = pl.ds(t * LANES, LANES)
-        load(wq.at[:, cols], wq_v.at[:, cols], t)
-        load(sq.at[:, cols], sq_v.at[:, cols], t)
-    load(wk, wkv_v.at[pl.ds(0, 32), :], KV_ROW)
-    load(sk, skv_v.at[pl.ds(0, 32), :], KV_ROW)
-    load(wv, wkv_v.at[pl.ds(32, 32), :], KV_ROW)
-    load(sv, skv_v.at[pl.ds(32, 32), :], KV_ROW)
-    load(norm_a, norm_v.at[0], NORM_ROW)
-    load(norm_b, norm_v.at[1], NORM_ROW)
+    barrier = pltpu.get_barrier_semaphore()
+    for device in ({"zero_0": right, "zero_1": 1}, {"zero_0": left, "zero_1": 1}):
+        pl.semaphore_signal(barrier, inc=1, device_id=device, device_id_type=MESH)
+
+    @pl.when(c == 0)
+    def _():
+        pl.semaphore_signal(barrier, inc=1, device_id=partner, device_id_type=MESH)
+
+    for row in (0, HALF):
+        load_rows(0, row, FIRST, 0)
+    for row in (FIRST, HALF + FIRST):
+        load_rows(0, row, HALF - FIRST, TILES)
+    load(wk, wkv_v.at[pl.ds(0, 32), :], KV_ROW + 1)
+    load(sk, skv_v.at[pl.ds(0, 32), :], KV_ROW + 1)
+    load(wv, wkv_v.at[pl.ds(32, 32), :], KV_ROW + 1)
+    load(sv, skv_v.at[pl.ds(32, 32), :], KV_ROW + 1)
+    load(norm_a, norm_v.at[0], NORM_ROW + 1)
+    load(norm_b, norm_v.at[1], NORM_ROW + 1)
+    for t in range(1, TILES):
+        load_rows(t, 0, ROWS, t)
+
+    @pl.when(c == 0)
+    def _():
+        for d in (2, 1, 3):
+            pl.semaphore_signal(barrier, inc=1, device_id={"width_1": lax.rem(y + d, 4)}, device_id_type=MESH)
+            pl.semaphore_signal(barrier, inc=1, device_id={"width_0": lax.rem(z + d, 4)}, device_id_type=MESH)
+
+    def wait_for_neighbours():
+        @pl.when(c == 1)
+        def _():
+            pl.semaphore_wait(barrier, 5)
+            pl.semaphore_signal(go.at[0], inc=1, device_id=partner, device_id_type=MESH)
+            for side in (left, right):
+                pl.semaphore_signal(vouch, inc=1, device_id={"zero_0": side}, device_id_type=MESH)
+
+        @pl.when(c == 0)
+        def _():
+            pl.semaphore_wait(go.at[0], 1)
+
+    def wait_for_far():
+        @pl.when(c == 1)
+        def _():
+            pl.semaphore_wait(vouch, 2)
+            pl.semaphore_signal(go.at[1], inc=1, device_id=partner, device_id_type=MESH)
+
+        @pl.when(c == 0)
+        def _():
+            pl.semaphore_wait(go.at[1], 1)
 
     def group_peer(d):
         other = lax.rem(me + d, 8)
         return {"zero_0": other // 2, "zero_1": lax.rem(other, 2)}
 
-    barrier = pltpu.get_barrier_semaphore()
-    for d in (2, 1, 3):
-        device = {"zero_0": lax.rem(x + d, 4), "zero_1": 1}
-        pl.semaphore_signal(barrier, inc=1, device_id=device, device_id_type=MESH)
-
-    @pl.when(c == 0)
-    def _():
-        pl.semaphore_signal(barrier, inc=1, device_id=partner, device_id_type=MESH)
-        for d in (2, 1, 3):
-            pl.semaphore_signal(barrier, inc=1, device_id={"width_1": lax.rem(y + d, 4)}, device_id_type=MESH)
-            pl.semaphore_signal(barrier, inc=1, device_id={"width_0": lax.rem(z + d, 4)}, device_id_type=MESH)
-
-    def wait_for_group():
-        @pl.when(c == 1)
-        def _():
-            pl.semaphore_wait(barrier, 7)
-            pl.semaphore_signal(go, inc=1, device_id=partner, device_id_type=MESH)
-
-        @pl.when(c == 0)
-        def _():
-            pl.semaphore_wait(go, 1)
+    nothing = jnp.zeros((8, LANES), jnp.float32)
+
+    def sum_rows(t, first, rows, carry):
+        cols = pl.ds(t * LANES, LANES)
+
+        def body(i, carry):
+            acc, top = carry
+            at = pl.ds(pl.multiple_of(first + i * 64, 64), 64)
+            r = mix(sq_v[at, cols], wq_v[at, cols])
+            res_q[at, cols] = r
+            size = jnp.abs(r).reshape(8, 8, LANES)
+            acc = acc + jnp.sum(size, axis=0)
+            return acc, jnp.maximum(top, jnp.max(size, axis=0)) if t == 0 else top
+
+        return lax.fori_loop(0, rows // 64, body, carry)
 
     def sum_tile(t):
         wait_bytes(wq_v.at[:, pl.ds(0, 2 * LANES)], in_sem.at[t])
-        cols = pl.ds(t * LANES, LANES)
-
-        def body(i, carry):
-            acc, top = carry
-            rows = pl.ds(pl.multiple_of(i * STEP, STEP), STEP)
-            r = mix(sq_v[rows, cols], wq_v[rows, cols])
-            res_q[rows, cols] = r
-            size = jnp.abs(r).reshape(STEP // 8, 8, LANES)
-            acc = acc + jnp.sum(size, axis=0)
-            return acc, jnp.maximum(top, jnp.max(size, axis=0)) if t == 0 else top
-
-        none = jnp.zeros((8, LANES), jnp.float32)
-        acc, top = lax.fori_loop(0, ROWS // STEP, body, (none, none))
+        acc, _ = sum_rows(t, 0, ROWS, (nothing, nothing))
         sums[me, t] = jnp.sum(acc, axis=0, keepdims=True)
-        return jnp.max(top, axis=0, keepdims=True)
+
+    def sum_first(part, acc):
+        row, rows = (0, FIRST) if part == 0 else (FIRST, HALF - FIRST)
+        wait_bytes(wq_v.at[pl.ds(0, rows), :], in_sem.at[part * TILES])
+        carry = (acc, nothing)
+        for half in range(2):
+            carry = sum_rows(0, half * HALF + row, rows, carry)
+        acc, top = carry
+        top = jnp.maximum(jnp.max(top, axis=0, keepdims=True), 1e-30)
+        sums[me, MAX_ROW + part] = top
+        return acc, CODE / top
 
     def send_sums():
         for d in (4, 5, 3, 2, 6, 7, 1):
@@ -175,7 +211,7 @@
 
     def decode_rows(origin, k, scale):
         _, row, rows, _ = UNITS[k]
-        own = sums[origin * 2 + c, MAX_ROW] * scale
+        own = sums[origin * 2 + c, MAX_ROW + (k % 3 > 0)] * scale
 
         def body(i, carry):
             at = pl.multiple_of(row + i * 64, 64)
@@ -188,17 +224,19 @@
     lane_of = lax.broadcasted_iota(jnp.int32, (KV, LANES), 1)
     diagonal = lane_of == lax.broadcasted_iota(jnp.int32, (KV, LANES), 0)
 
-    top = jnp.maximum(sum_tile(0), 1e-30)
-    sums[me, MAX_ROW] = top
-    scale = CODE / top
+    acc, scale = sum_first(0, nothing)
     encode_rows(0, scale)
-    encode_rows(2, scale)
-    wait_for_group()
+    encode_rows(3, scale)
+    wait_for_neighbours()
     send_right(0)
-    send_left(2)
-    for t in range(1, TILES):
-        sum_tile(t)
-    wait_bytes(wq_v.at[pl.ds(0, 4 * 32 * ROWS // COLS), :], in_sem.at[KV_ROW])
+    send_left(3)
+    acc, scale = sum_first(1, acc)
+    encode_rows(1, scale)
+    send_right(1)
+    encode_rows(4, scale)
+    send_left(4)
+    sums[me, 0] = jnp.sum(acc, axis=0, keepdims=True)
+    wait_bytes(wq_v.at[pl.ds(0, 4 * 32 * ROWS // COLS), :], in_sem.at[KV_ROW + 1])
     acc = jnp.zeros((KV, LANES), jnp.float32)
     for j in range(ROWS // LANES):
         cols = pl.ds(j * LANES, LANES)
@@ -207,16 +245,19 @@
         acc = acc + jnp.abs(r)
     row_sums = jnp.sum(acc, axis=1, keepdims=True)
     sums[me, KV_ROW] = jnp.sum(jnp.where(diagonal, row_sums, 0.0), axis=0, keepdims=True)
-    wait_bytes(norm_v, in_sem.at[NORM_ROW])
+    wait_bytes(norm_v, in_sem.at[NORM_ROW + 1])
     own_norm = norm_v[0] + norm_v[1]
     sums[me, NORM_ROW] = jnp.concatenate([own_norm, own_norm], axis=1)
+    for t in range(1, TILES):
+        sum_tile(t)
+    wait_for_far()
     send_sums()
-    encode_rows(1, scale)
-    send_right(1)
-    encode_rows(3, scale)
-    for k in (3, 0, 1):
+    encode_rows(2, scale)
+    send_right(2)
+    encode_rows(5, scale)
+    for k in (5, 0, 1, 2):
         send_left(k)
-    for k in (2, 3):
+    for k in (3, 4, 5):
         send_right(k)
 
     def factor_of(t):
@@ -252,7 +293,7 @@
                     at = half * HALF + j * LANES
                     there = pl.ds(pl.multiple_of(me * ROWS + at, LANES), LANES)
                     out_kv[:, there] = (res_kv[:, pl.ds(at, LANES)] * scale).astype(jnp.bfloat16)
-            k = len(CODED) + 2 * (t - 1) + half
+            k = len(CODED) + 2 * t - 2 + half
             for go_there in (send_right, send_left) if half == 0 else (send_left, send_right):
                 go_there(k)
             relay(x, k)
@@ -324,7 +365,7 @@
             pl.when(c == 0)(norm_steps[i])
     pl.when(c == 0)(lambda: norm_to_partner().wait_send())
     pl.when(c == 1)(lambda: norm_to_partner().wait_recv())
-    for k in (0, 2, 1, 3, *range(len(CODED), len(UNITS))):
+    for k in (0, 3, 1, 4, 2, 5, *range(len(CODED), len(UNITS))):
         unit_copy(place(far, k), far_recv.at[k], partner).wait_recv()
         hand_on(far, k)
 
@@ -338,27 +379,22 @@
     out_q, out_kv, res_q, res_kv, fac_q, fac_k, fac_v, norm,
     final_q, final_k, final_v, factor_q, factor_k, factor_v, serve_norm, result_q, result_k, result_v, sem,
 ):
-    copies = []
-
-    def write(src, dst):
-        copy = pltpu.make_async_copy(src, dst, sem.at[len(copies)])
-        copy.start()
-        copies.append(copy)
-
+    def write(src, dst, which):
+        pltpu.make_async_copy(src, dst, sem.at[which]).start()
+
+    small = ((fac_q, factor_q), (fac_k, factor_k), (fac_v, factor_v), (norm, serve_norm))
+    for i, (src, dst) in enumerate(small):
+        write(src, dst, i)
     for part in range(8):
         rows = pl.ds(part * ROWS, ROWS)
-        write(out_q.at[rows, :], final_q.at[rows, :])
-    write(res_q, result_q)
-    write(out_kv.at[pl.ds(0, 32), :], final_k)
-    write(out_kv.at[pl.ds(32, 32), :], final_v)
-    write(res_kv.at[pl.ds(0, 32), :], result_k)
-    write(res_kv.at[pl.ds(32, 32), :], result_v)
-    write(fac_q, factor_q)
-    write(fac_k, factor_k)
-    write(fac_v, factor_v)
-    write(norm, serve_norm)
-    for copy in copies:
-        copy.wait()
+        write(out_q.at[rows, :], final_q.at[rows, :], 4)
+    write(res_q, result_q, 5)
+    write(out_kv.at[pl.ds(0, 32), :], final_k, 6)
+    write(out_kv.at[pl.ds(32, 32), :], final_v, 6)
+    write(res_kv.at[pl.ds(0, 32), :], result_k, 7)
+    write(res_kv.at[pl.ds(32, 32), :], result_v, 7)
+    for i, ref in enumerate((fac_q, fac_k, fac_v, norm, out_q, res_q, out_kv, res_kv)):
+        pltpu.make_async_copy(ref, ref, sem.at[i]).wait()
 
 
 def on_device(weight_query, smooth_query, weight_key, smooth_key, weight_value, smooth_value, norm_train, norm_step):
@@ -392,7 +428,7 @@
             pltpu.VMEM((4, 8, LANES), f32),
             pltpu.VMEM((4, 2, 8, LANES), f32),
             pltpu.VMEM((64, LANES), f32),
-            dma((SUM_ROWS,)),
+            dma((NORM_ROW + 2,)),
             dma,
             dma,
             dma,
@@ -401,6 +437,7 @@
             dma,
             dma((3,)),
             dma((3,)),
+            pltpu.SemaphoreType.REGULAR((2,)),
             pltpu.SemaphoreType.REGULAR,
         ],
         compiler_params=pltpu.CompilerParams(
@@ -433,7 +470,7 @@
         out_shape=tuple(jax.ShapeDtypeStruct(shape, dtype) for shape, dtype in outs),
         in_specs=[vmem_spec] * len(held),
         out_specs=tuple(any_spec for _ in outs),
-        scratch_shapes=[dma((17,))],
+        scratch_shapes=[dma((8,))],
         compiler_params=pltpu.CompilerParams(vmem_limit_bytes=4 * 1024 * 1024),
         name="write",
     )(*gathered)

time: 51.7 us -> 51.2 us (level)
  no operation moved by 1% of the time
where the time goes in v5:
time: 51.2 us; the launch traced here: 51.1 us
  Pallas kernels  50.5 us (99%)
  between operations  0.65 us (1%)
    pallas_call x1, Pallas kernels, on_device(): pl.pallas_call(gather_kernel, out_shape=tuple((pltpu.VMEM(shape, dtype) f...  46.1 us
    pallas_call x1, Pallas kernels, on_device(): pl.pallas_call(write_kernel, out_shape=tuple((jax.ShapeDtypeStruct(shape,...  4.38 us

profile of v5, /device:TPU:1, one launch (start us, length us, event | category | flops | bytes accessed | tf_op | source)
XLA Modules:
  0.0 51.1 jit_solution(4104020283120611184)
XLA Ops:
  0.6 46.1 %gather.1 = (bf16[8192,512]{1,0:T(8,128)(2,1)S(1)}, bf16[64,8192]{1,0:T(8,128)(2,1)S(1)}, f32[1024,512]{1,0:T(8,128)S(1)}, f32[64,1024]{1,0:T(8,128)S(1)}, f32[1...) custom-call(f32[1024,512]{1,0:T(8,128)} %wq.1, f32[1024,512]{1,0:T(8,128)} %sq.1, ...), custom_call_target="tpu_custom_call" | custom-call | tf_op jit(solution)/shard_map/gather/pallas_call | solution.py:415
  46.7 4.4 %write.1 = (bf16[8192,512]{1,0:T(8,128)(2,1)}, bf16[32,8192]{1,0:T(8,128)(2,1)}, bf16[32,8192]{1,0:T(8,128)(2,1)}, f32[1,512]{1,0:T(1,128)}, f32[1,32]{1,0:T(1,1...) custom-call(bf16[8192,512]{1,0:T(8,128)(2,1)S(1)} %get-tuple-element, ...), custom_call_target="tpu_custom_call" | custom-call | tf_op jit(solution)/shard_map/write/pallas_call | solution.py:468

commit v6 on v5

--- a/solution.py
+++ b/solution.py
@@ -28,10 +28,11 @@
 PIECES = ((0, FIRST), (192, 128), (320, 192))
 CODED = tuple((0, half * HALF + row, rows, half) for half in range(2) for row, rows in PIECES)
 UNITS = CODED + tuple((tile, half * HALF, HALF, half) for tile in range(1, TILES + 1) for half in range(2))
-ORDER = (
-    (0, 1, 2, 3, 4, 5, *range(6, len(UNITS))),
-    (3, 4, 5, 0, 1, 2, *range(6, len(UNITS))),
-)
+KV_UNITS = (len(UNITS) - 2, len(UNITS) - 1)
+SIDE_GROUPS = ((0, 1, 2), (3, 4, 5), *((k, k + 1) for k in range(6, len(UNITS), 2)))
+FAR_GROUPS = ((0, 1, 2), (3, 4, 5), (6, 8), (7, 9), (10,), (11,), (12,), (13,))
+SIDE_OF = {k: g for g, units in enumerate(SIDE_GROUPS) for k in units}
+FAR_OF = {k: g for g, units in enumerate(FAR_GROUPS) for k in units}
 CODE = 180.0
 
 
@@ -58,7 +59,8 @@
     wq, sq, wk, sk, wv, sv, norm_a, norm_b,
     out_q, out_kv, res_q, res_kv, fac_q, fac_k, fac_v, norm_out,
     wq_v, sq_v, wkv_v, skv_v, norm_v, coded, sums, norm_y, norm_z, norm_all,
-    in_sem, send_sem, sum_send, sum_recv, side_recv, far_recv, rel_recv, norm_send, norm_recv, go, vouch,
+    in_sem, send_sem, extra_send, sum_send, sum_recv, side_recv, far_recv, rel_recv, kv_recv, far_kv_recv,
+    norm_send, norm_recv, go, vouch,
 ):
     x, c = lax.axis_index("zero_0"), lax.axis_index("zero_1")
     z, y = lax.axis_index("width_0"), lax.axis_index("width_1")
@@ -173,31 +175,36 @@
                 device_id_type=MESH,
             ).start()
 
-    def final_place(origin, k):
+    def final_place(origin, k, core):
         tile, row, rows, _ = UNITS[k]
+        at = (origin * 2 + core) * ROWS + row
         if tile < TILES:
-            return out_q.at[pl.ds(pl.multiple_of((origin * 2 + c) * ROWS + row, 64), rows), pl.ds(tile * LANES, LANES)]
-        return out_kv.at[:, pl.ds(pl.multiple_of((origin * 2 + c) * ROWS + row, HALF), rows)]
+            return out_q.at[pl.ds(pl.multiple_of(at, 64), rows), pl.ds(tile * LANES, LANES)]
+        return out_kv.at[:, pl.ds(pl.multiple_of(at, HALF), rows)]
 
     def place(origin, k):
         _, row, rows, _ = UNITS[k]
-        return coded.at[origin, pl.ds(row, rows)] if k < len(CODED) else final_place(origin, k)
-
-    def unit_copy(ref, recv_sem, device):
+        return coded.at[origin, pl.ds(row, rows)] if k < len(CODED) else final_place(origin, k, c)
+
+    def unit_copy(ref, recv_sem, device, sem=send_sem):
         return pltpu.make_async_remote_copy(
-            src_ref=ref, dst_ref=ref, send_sem=send_sem, recv_sem=recv_sem, device_id=device, device_id_type=MESH
+            src_ref=ref, dst_ref=ref, send_sem=sem, recv_sem=recv_sem, device_id=device, device_id_type=MESH
         )
 
+    def wait_units(units, sem):
+        rows = sum(64 * HALF // LANES if k >= KV_UNITS[0] else UNITS[k][2] for k in units)
+        wait_bytes(out_q.at[pl.ds(0, rows), pl.ds(0, LANES)], sem)
+
     to_right, to_left = {"zero_0": right}, {"zero_0": left}
 
     def send_right(k):
-        unit_copy(place(x, k), side_recv.at[0, k], to_right).start()
+        unit_copy(place(x, k), side_recv.at[0, SIDE_OF[k]], to_right).start()
 
     def send_left(k):
-        unit_copy(place(x, k), side_recv.at[1, k], to_left).start()
+        unit_copy(place(x, k), side_recv.at[1, SIDE_OF[k]], to_left).start()
 
     def relay(origin, k):
-        unit_copy(final_place(origin, k), rel_recv, partner).start()
+        unit_copy(final_place(origin, k, c), rel_recv, partner).start()
 
     def encode_rows(k, scale):
         _, row, rows, _ = UNITS[k]
@@ -347,32 +354,79 @@
         return norm_copy(norm_out, pl.ds(0, 64), 2, partner)
 
     far = lax.rem(x + 2, 4)
-    norm_steps = {2: norm_along_y, 4: norm_along_z, 6: norm_end, 7: lambda: norm_to_partner().start()}
+    norm_steps = {1: norm_along_y, 2: norm_along_z, 3: norm_end, 4: lambda: norm_to_partner().start()}
 
     def hand_on(origin, k):
         if k < len(CODED):
             decode_rows(origin, k, first_scale)
         relay(origin, k)
 
-    for i in range(len(UNITS)):
+    def forward(origin, k):
+        unit_copy(place(origin, k), far_recv.at[FAR_OF[k]], to_left if UNITS[k][3] else to_right).start()
+
+    for i in range(len(SIDE_GROUPS)):
         for side in range(2):
-            k, origin = ORDER[side][i], left if side == 0 else right
-            unit_copy(place(origin, k), side_recv.at[side, k], partner).wait_recv()
-            if UNITS[k][3] == side:
-                unit_copy(place(origin, k), far_recv.at[k], to_right if side == 0 else to_left).start()
-            hand_on(origin, k)
+            group = i if i > 1 or side == 0 else 1 - i
+            units, origin = SIDE_GROUPS[group], left if side == 0 else right
+            wait_units(units, side_recv.at[side, group])
+            for k in units:
+                if UNITS[k][3] == side and k in KV_UNITS:
+
+                    @pl.when(c == 1)
+                    def _():
+                        forward(origin, k)
+                        relay(origin, k)
+
+                    @pl.when(c == 0)
+                    def _():
+                        unit_copy(final_place(origin, k, 0), kv_recv.at[side], partner).start()
+                    continue
+                if UNITS[k][3] == side:
+                    forward(origin, k)
+                hand_on(origin, k)
         if i in norm_steps:
             pl.when(c == 0)(norm_steps[i])
+
+    @pl.when(c == 1)
+    def _():
+        for side, origin, device in ((0, left, to_right), (1, right, to_left)):
+            k = KV_UNITS[side]
+            wait_units((k,), kv_recv.at[side])
+            unit_copy(final_place(origin, k, 0), far_kv_recv.at[side], device, extra_send).start()
+
     pl.when(c == 0)(lambda: norm_to_partner().wait_send())
     pl.when(c == 1)(lambda: norm_to_partner().wait_recv())
-    for k in (0, 3, 1, 4, 2, 5, *range(len(CODED), len(UNITS))):
-        unit_copy(place(far, k), far_recv.at[k], partner).wait_recv()
-        hand_on(far, k)
-
-    shard_rows = ROWS + KV * ROWS // COLS
+    for group, units in enumerate(FAR_GROUPS):
+        if units[0] in KV_UNITS:
+            continue
+        wait_units(units, far_recv.at[group])
+        for k in units:
+            hand_on(far, k)
+
+    @pl.when(c == 1)
+    def _():
+        for k in KV_UNITS:
+            wait_units((k,), far_recv.at[FAR_OF[k]])
+            relay(far, k)
+        for side, k in enumerate(KV_UNITS):
+            wait_units((k,), far_kv_recv.at[side])
+            unit_copy(final_place(far, k, 0), rel_recv, partner, extra_send).start()
+
+    share = ROWS + KV * ROWS // COLS
+    kv_rows = KV * ROWS // COLS
+
     wait_bytes(sums.at[pl.ds(0, 7)], sum_send)
-    wait_bytes(out_q.at[pl.ds(0, 7 * shard_rows), :], send_sem)
-    wait_bytes(out_q.at[pl.ds(0, 4 * shard_rows), :], rel_recv)
+
+    @pl.when(c == 1)
+    def _():
+        wait_bytes(out_q.at[pl.ds(0, 7 * share), :], send_sem)
+        wait_bytes(out_q.at[pl.ds(0, 2 * kv_rows), :], extra_send)
+        wait_bytes(out_q.at[pl.ds(0, 4 * share - 2 * kv_rows), :], rel_recv)
+
+    @pl.when(c == 0)
+    def _():
+        wait_bytes(out_q.at[pl.ds(0, 7 * share - 2 * kv_rows), :], send_sem)
+        wait_bytes(out_q.at[pl.ds(0, 4 * share + kv_rows), :], rel_recv)
 
 
 def write_kernel(
@@ -410,7 +464,6 @@
         ((1, 32), f32),
         ((64, LANES), bf16),
     )
-    units = len(UNITS)
     dma = pltpu.SemaphoreType.DMA
     gathered = pl.pallas_call(
         gather_kernel,
@@ -432,9 +485,12 @@
             dma,
             dma,
             dma,
-            dma((2, units)),
-            dma((units,)),
             dma,
+            dma((2, len(SIDE_GROUPS))),
+            dma((len(FAR_GROUPS),)),
+            dma,
+            dma((2,)),
+            dma((2,)),
             dma((3,)),
             dma((3,)),
             pltpu.SemaphoreType.REGULAR((2,)),

time: 51.2 us -> 50.5 us (0.986)
  Pallas kernels: 50.5 us -> 49.8 us
    pallas_call x1, Pallas kernels: 46.1 us -> 45.4 us  [on_device(): pl.pallas_call(gather_kernel, out_shape=tuple((pltpu.VMEM(shape, dtype) f...]
where the time goes in v6:
time: 50.5 us; the launch traced here: 50.4 us
  Pallas kernels  49.8 us (99%)
  between operations  0.65 us (1%)
    pallas_call x1, Pallas kernels, on_device(): pl.pallas_call(gather_kernel, out_shape=tuple((pltpu.VMEM(shape, dtype) f...  45.4 us
    pallas_call x1, Pallas kernels, on_device(): pl.pallas_call(write_kernel, out_shape=tuple((jax.ShapeDtypeStruct(shape,...  4.38 us

profile of v6, /device:TPU:1, one launch (start us, length us, event | category | flops | bytes accessed | tf_op | source)
XLA Modules:
  0.0 50.4 jit_solution(4664530727070107258)
XLA Ops:
  0.6 45.4 %gather.1 = (bf16[8192,512]{1,0:T(8,128)(2,1)S(1)}, bf16[64,8192]{1,0:T(8,128)(2,1)S(1)}, f32[1024,512]{1,0:T(8,128)S(1)}, f32[64,1024]{1,0:T(8,128)S(1)}, f32[1...) custom-call(f32[1024,512]{1,0:T(8,128)} %wq.1, f32[1024,512]{1,0:T(8,128)} %sq.1, ...), custom_call_target="tpu_custom_call" | custom-call | tf_op jit(solution)/shard_map/gather/pallas_call | solution.py:468
  46.1 4.4 %write.1 = (bf16[8192,512]{1,0:T(8,128)(2,1)}, bf16[32,8192]{1,0:T(8,128)(2,1)}, bf16[32,8192]{1,0:T(8,128)(2,1)}, f32[1,512]{1,0:T(1,128)}, f32[1,32]{1,0:T(1,1...) custom-call(bf16[8192,512]{1,0:T(8,128)(2,1)S(1)} %get-tuple-element, ...), custom_call_target="tpu_custom_call" | custom-call | tf_op jit(solution)/shard_map/write/pallas_call | solution.py:524

commit v7 on v6

--- a/solution.py
+++ b/solution.py
@@ -21,16 +21,25 @@
 LANES = 128
 TILES = COLS // LANES
 STEP = 128
+STEPS = {96: 96, 288: 96, 128: 128, 416: 104, ROWS: STEP}
 KV_ROW, NORM_ROW, MAX_ROW = TILES, TILES + 1, TILES + 2
+ROW_OF = (1, 0, 2, 3, KV_ROW)
 SUM_ROWS = TILES + 4
 
-FIRST = 192
-PIECES = ((0, FIRST), (192, 128), (320, 192))
+FIRST = 96
+PIECES = ((0, FIRST), (FIRST, 288), (384, 128))
 CODED = tuple((0, half * HALF + row, rows, half) for half in range(2) for row, rows in PIECES)
-UNITS = CODED + tuple((tile, half * HALF, HALF, half) for tile in range(1, TILES + 1) for half in range(2))
+QUARTER = HALF // 2
+UNITS = (
+    *CODED,
+    *((tile, half * HALF, HALF, half) for tile in range(1, TILES - 1) for half in range(2)),
+    *((TILES - 1, part * QUARTER, QUARTER, part // 2) for part in range(4)),
+    *((TILES, half * HALF, HALF, half) for half in range(2)),
+)
+FIRST_OF = tuple(min(k for k, unit in enumerate(UNITS) if unit[0] == tile) for tile in range(TILES + 1))
 KV_UNITS = (len(UNITS) - 2, len(UNITS) - 1)
-SIDE_GROUPS = ((0, 1, 2), (3, 4, 5), *((k, k + 1) for k in range(6, len(UNITS), 2)))
-FAR_GROUPS = ((0, 1, 2), (3, 4, 5), (6, 8), (7, 9), (10,), (11,), (12,), (13,))
+SIDE_GROUPS = ((0, 1, 2), (3, 4, 5), (6, 7, 8, 9), (10, 11, 12, 13, 14, 15))
+FAR_GROUPS = ((0, 1, 2), (3, 4, 5), (6, 8), (7, 9), (10,), (12,), (11,), (13,), (14,), (15,))
 SIDE_OF = {k: g for g, units in enumerate(SIDE_GROUPS) for k in units}
 FAR_OF = {k: g for g, units in enumerate(FAR_GROUPS) for k in units}
 CODE = 180.0
@@ -91,13 +100,14 @@
         load_rows(0, row, FIRST, 0)
     for row in (FIRST, HALF + FIRST):
         load_rows(0, row, HALF - FIRST, TILES)
+    load_rows(1, 0, ROWS, 1)
     load(wk, wkv_v.at[pl.ds(0, 32), :], KV_ROW + 1)
     load(sk, skv_v.at[pl.ds(0, 32), :], KV_ROW + 1)
     load(wv, wkv_v.at[pl.ds(32, 32), :], KV_ROW + 1)
     load(sv, skv_v.at[pl.ds(32, 32), :], KV_ROW + 1)
     load(norm_a, norm_v.at[0], NORM_ROW + 1)
     load(norm_b, norm_v.at[1], NORM_ROW + 1)
-    for t in range(1, TILES):
+    for t in range(2, TILES):
         load_rows(t, 0, ROWS, t)
 
     @pl.when(c == 0)
@@ -136,22 +146,23 @@
 
     def sum_rows(t, first, rows, carry):
         cols = pl.ds(t * LANES, LANES)
+        step = STEPS[rows]
 
         def body(i, carry):
             acc, top = carry
-            at = pl.ds(pl.multiple_of(first + i * 64, 64), 64)
+            at = pl.ds(pl.multiple_of(first + i * step, 8), step)
             r = mix(sq_v[at, cols], wq_v[at, cols])
             res_q[at, cols] = r
-            size = jnp.abs(r).reshape(8, 8, LANES)
+            size = jnp.abs(r).reshape(step // 8, 8, LANES)
             acc = acc + jnp.sum(size, axis=0)
             return acc, jnp.maximum(top, jnp.max(size, axis=0)) if t == 0 else top
 
-        return lax.fori_loop(0, rows // 64, body, carry)
+        return lax.fori_loop(0, rows // step, body, carry)
 
     def sum_tile(t):
         wait_bytes(wq_v.at[:, pl.ds(0, 2 * LANES)], in_sem.at[t])
         acc, _ = sum_rows(t, 0, ROWS, (nothing, nothing))
-        sums[me, t] = jnp.sum(acc, axis=0, keepdims=True)
+        sums[me, ROW_OF[t]] = jnp.sum(acc, axis=0, keepdims=True)
 
     def sum_first(part, acc):
         row, rows = (0, FIRST) if part == 0 else (FIRST, HALF - FIRST)
@@ -164,13 +175,13 @@
         sums[me, MAX_ROW + part] = top
         return acc, CODE / top
 
-    def send_sums():
+    def send_sums(first, count, which):
         for d in (4, 5, 3, 2, 6, 7, 1):
             pltpu.make_async_remote_copy(
-                src_ref=sums.at[me],
-                dst_ref=sums.at[me],
+                src_ref=sums.at[me, pl.ds(first, count)],
+                dst_ref=sums.at[me, pl.ds(first, count)],
                 send_sem=sum_send,
-                recv_sem=sum_recv,
+                recv_sem=sum_recv.at[which],
                 device_id=group_peer(d),
                 device_id_type=MESH,
             ).start()
@@ -179,8 +190,13 @@
         tile, row, rows, _ = UNITS[k]
         at = (origin * 2 + core) * ROWS + row
         if tile < TILES:
-            return out_q.at[pl.ds(pl.multiple_of(at, 64), rows), pl.ds(tile * LANES, LANES)]
+            return out_q.at[pl.ds(pl.multiple_of(at, 32), rows), pl.ds(tile * LANES, LANES)]
         return out_kv.at[:, pl.ds(pl.multiple_of(at, HALF), rows)]
+
+    def kv_part(origin, k, last):
+        first, columns = (LANES, HALF - LANES) if last else (0, LANES)
+        at = origin * 2 * ROWS + UNITS[k][1] + first
+        return out_kv.at[:, pl.ds(pl.multiple_of(at, LANES), columns)]
 
     def place(origin, k):
         _, row, rows, _ = UNITS[k]
@@ -208,25 +224,27 @@
 
     def encode_rows(k, scale):
         _, row, rows, _ = UNITS[k]
+        step = STEPS[rows]
 
         def body(i, carry):
-            at = pl.ds(pl.multiple_of(row + i * 64, 64), 64)
+            at = pl.ds(pl.multiple_of(row + i * step, 16), step)
             coded[x, at, :] = encode(res_q[at, 0:LANES], scale)
             return carry
 
-        lax.fori_loop(0, rows // 64, body, 0)
+        lax.fori_loop(0, rows // step, body, 0)
 
     def decode_rows(origin, k, scale):
         _, row, rows, _ = UNITS[k]
+        step = STEPS[rows]
         own = sums[origin * 2 + c, MAX_ROW + (k % 3 > 0)] * scale
 
         def body(i, carry):
-            at = pl.multiple_of(row + i * 64, 64)
-            there = pl.ds(pl.multiple_of((origin * 2 + c) * ROWS + at, 64), 64)
-            out_q[there, 0:LANES] = (decode(coded[origin, pl.ds(at, 64), :]) * own).astype(jnp.bfloat16)
+            at = pl.multiple_of(row + i * step, 16)
+            there = pl.ds(pl.multiple_of((origin * 2 + c) * ROWS + at, 16), step)
+            out_q[there, 0:LANES] = (decode(coded[origin, pl.ds(at, step), :]) * own).astype(jnp.bfloat16)
             return carry
 
-        lax.fori_loop(0, rows // 64, body, 0)
+        lax.fori_loop(0, rows // step, body, 0)
 
     lane_of = lax.broadcasted_iota(jnp.int32, (KV, LANES), 1)
     diagonal = lane_of == lax.broadcasted_iota(jnp.int32, (KV, LANES), 0)
@@ -242,7 +260,14 @@
     send_right(1)
     encode_rows(4, scale)
     send_left(4)
-    sums[me, 0] = jnp.sum(acc, axis=0, keepdims=True)
+    sum_tile(1)
+    wait_for_far()
+    send_sums(0, 1, 0)
+    encode_rows(2, scale)
+    send_right(2)
+    encode_rows(5, scale)
+    send_left(5)
+    sums[me, ROW_OF[0]] = jnp.sum(acc, axis=0, keepdims=True)
     wait_bytes(wq_v.at[pl.ds(0, 4 * 32 * ROWS // COLS), :], in_sem.at[KV_ROW + 1])
     acc = jnp.zeros((KV, LANES), jnp.float32)
     for j in range(ROWS // LANES):
@@ -255,22 +280,18 @@
     wait_bytes(norm_v, in_sem.at[NORM_ROW + 1])
     own_norm = norm_v[0] + norm_v[1]
     sums[me, NORM_ROW] = jnp.concatenate([own_norm, own_norm], axis=1)
-    for t in range(1, TILES):
+    for t in range(2, TILES):
         sum_tile(t)
-    wait_for_far()
-    send_sums()
-    encode_rows(2, scale)
-    send_right(2)
-    encode_rows(5, scale)
-    for k in (5, 0, 1, 2):
+    send_sums(1, SUM_ROWS - 1, 1)
+    for k in (0, 1, 2):
         send_left(k)
     for k in (3, 4, 5):
         send_right(k)
 
     def factor_of(t):
-        total = sums[0, t]
+        total = sums[0, ROW_OF[t]]
         for other in range(1, 8):
-            total = total + sums[other, t]
+            total = total + sums[other, ROW_OF[t]]
         return total * (1.0 / D_MODEL)
 
     def narrow_tile(t):
@@ -300,13 +321,16 @@
                     at = half * HALF + j * LANES
                     there = pl.ds(pl.multiple_of(me * ROWS + at, LANES), LANES)
                     out_kv[:, there] = (res_kv[:, pl.ds(at, LANES)] * scale).astype(jnp.bfloat16)
-            k = len(CODED) + 2 * t - 2 + half
-            for go_there in (send_right, send_left) if half == 0 else (send_left, send_right):
-                go_there(k)
-            relay(x, k)
-
-    wait_bytes(sums.at[pl.ds(0, 7)], sum_recv)
-    for t in range(1, TILES + 1):
+            for k in range(FIRST_OF[t], len(UNITS)):
+                if UNITS[k][0] == t and UNITS[k][3] == half:
+                    for go_there in (send_right, send_left) if half == 0 else (send_left, send_right):
+                        go_there(k)
+                    relay(x, k)
+
+    wait_bytes(sums.at[pl.ds(0, 7), pl.ds(0, 1)], sum_recv.at[0])
+    narrow_tile(1)
+    wait_bytes(sums.at[pl.ds(0, 7), pl.ds(1, SUM_ROWS - 1)], sum_recv.at[1])
+    for t in range(2, TILES + 1):
         narrow_tile(t)
     first_factor = factor_of(0)
     fac_q[:, 0:LANES] = first_factor
@@ -319,7 +343,7 @@
         return pltpu.make_async_remote_copy(
             src_ref=buf.at[at],
             dst_ref=buf.at[at],
-            send_sem=norm_send.at[stage],
+            send_sem=norm_send,
             recv_sem=norm_recv.at[stage],
             device_id=device,
             device_id_type=MESH,
@@ -347,14 +371,15 @@
                 for other in range(8):
                     norm_all[pl.ds(other * 8 + zz * 2 + pair, 1), :] = norm_z[zz, pair, pl.ds(other, 1), :]
         norm_out[...] = norm_all[...].astype(jnp.bfloat16)
-        wait_bytes(norm_y.at[pl.ds(0, 3)], norm_send.at[0])
-        wait_bytes(norm_z.at[pl.ds(0, 3)], norm_send.at[1])
+
+    def norm_give():
+        norm_to_partner().start()
 
     def norm_to_partner():
         return norm_copy(norm_out, pl.ds(0, 64), 2, partner)
 
     far = lax.rem(x + 2, 4)
-    norm_steps = {1: norm_along_y, 2: norm_along_z, 3: norm_end, 4: lambda: norm_to_partner().start()}
+    norm_steps = {1: norm_along_y, 2: norm_along_z, 3: norm_end}
 
     def hand_on(origin, k):
         if k < len(CODED):
@@ -379,7 +404,7 @@
 
                     @pl.when(c == 0)
                     def _():
-                        unit_copy(final_place(origin, k, 0), kv_recv.at[side], partner).start()
+                        unit_copy(final_place(origin, k, 0), kv_recv, partner).start()
                     continue
                 if UNITS[k][3] == side:
                     forward(origin, k)
@@ -389,12 +414,16 @@
 
     @pl.when(c == 1)
     def _():
+        wait_units(KV_UNITS, kv_recv)
         for side, origin, device in ((0, left, to_right), (1, right, to_left)):
             k = KV_UNITS[side]
-            wait_units((k,), kv_recv.at[side])
-            unit_copy(final_place(origin, k, 0), far_kv_recv.at[side], device, extra_send).start()
-
-    pl.when(c == 0)(lambda: norm_to_partner().wait_send())
+            unit_copy(kv_part(origin, k, False), far_kv_recv.at[0], device, extra_send).start()
+            for core in range(2):
+                to = {**device, "zero_1": core}
+                unit_copy(kv_part(origin, k, True), far_kv_recv.at[1], to, extra_send).start()
+
+    pl.when(c == 0)(norm_give)
+    pl.when(c == 0)(lambda: wait_bytes(out_q.at[pl.ds(0, 9 * 16 + 64), pl.ds(0, LANES)], norm_send))
     pl.when(c == 1)(lambda: norm_to_partner().wait_recv())
     for group, units in enumerate(FAR_GROUPS):
         if units[0] in KV_UNITS:
@@ -408,9 +437,11 @@
         for k in KV_UNITS:
             wait_units((k,), far_recv.at[FAR_OF[k]])
             relay(far, k)
-        for side, k in enumerate(KV_UNITS):
-            wait_units((k,), far_kv_recv.at[side])
-            unit_copy(final_place(far, k, 0), rel_recv, partner, extra_send).start()
+        wait_bytes(out_kv.at[:, pl.ds(0, 2 * LANES)], far_kv_recv.at[0])
+        for k in KV_UNITS:
+            unit_copy(kv_part(far, k, False), rel_recv, partner, extra_send).start()
+
+    wait_bytes(out_kv.at[:, pl.ds(0, 2 * (HALF - LANES))], far_kv_recv.at[1])
 
     share = ROWS + KV * ROWS // COLS
     kv_rows = KV * ROWS // COLS
@@ -426,7 +457,7 @@
     @pl.when(c == 0)
     def _():
         wait_bytes(out_q.at[pl.ds(0, 7 * share - 2 * kv_rows), :], send_sem)
-        wait_bytes(out_q.at[pl.ds(0, 4 * share + kv_rows), :], rel_recv)
+        wait_bytes(out_q.at[pl.ds(0, 4 * share + kv_rows // 4), :], rel_recv)
 
 
 def write_kernel(
@@ -485,13 +516,13 @@
             dma,
             dma,
             dma,
-            dma,
+            dma((2,)),
             dma((2, len(SIDE_GROUPS))),
             dma((len(FAR_GROUPS),)),
             dma,
+            dma,
             dma((2,)),
-            dma((2,)),
-            dma((3,)),
+            dma,
             dma((3,)),
             pltpu.SemaphoreType.REGULAR((2,)),
             pltpu.SemaphoreType.REGULAR,

time: 50.5 us -> 50.4 us (level)
  no operation moved by 1% of the time
where the time goes in v7:
time: 50.4 us; the launch traced here: 50.3 us
  Pallas kernels  49.6 us (98%)
  between operations  0.65 us (1%)
    pallas_call x1, Pallas kernels, on_device(): pl.pallas_call(gather_kernel, out_shape=tuple((pltpu.VMEM(shape, dtype) f...  45.2 us
    pallas_call x1, Pallas kernels, on_device(): pl.pallas_call(write_kernel, out_shape=tuple((jax.ShapeDtypeStruct(shape,...  4.38 us

profile of v7, /device:TPU:1, one launch (start us, length us, event | category | flops | bytes accessed | tf_op | source)
XLA Modules:
  0.0 50.3 jit_solution(10463036713821933743)
XLA Ops:
  0.6 45.2 %gather.1 = (bf16[8192,512]{1,0:T(8,128)(2,1)S(1)}, bf16[64,8192]{1,0:T(8,128)(2,1)S(1)}, f32[1024,512]{1,0:T(8,128)S(1)}, f32[64,1024]{1,0:T(8,128)S(1)}, f32[1...) custom-call(f32[1024,512]{1,0:T(8,128)} %wq.1, f32[1024,512]{1,0:T(8,128)} %sq.1, ...), custom_call_target="tpu_custom_call" | custom-call | tf_op jit(solution)/shard_map/gather/pallas_call | solution.py:499
  45.9 4.4 %write.1 = (bf16[8192,512]{1,0:T(8,128)(2,1)}, bf16[32,8192]{1,0:T(8,128)(2,1)}, bf16[32,8192]{1,0:T(8,128)(2,1)}, f32[1,512]{1,0:T(1,128)}, f32[1,32]{1,0:T(1,1...) custom-call(bf16[8192,512]{1,0:T(8,128)(2,1)S(1)} %get-tuple-element, ...), custom_call_target="tpu_custom_call" | custom-call | tf_op jit(solution)/shard_map/write/pallas_call | solution.py:555

commit v8 on v7

--- a/solution.py
+++ b/solution.py
@@ -21,25 +21,26 @@
 LANES = 128
 TILES = COLS // LANES
 STEP = 128
-STEPS = {96: 96, 288: 96, 128: 128, 416: 104, ROWS: STEP}
 KV_ROW, NORM_ROW, MAX_ROW = TILES, TILES + 1, TILES + 2
-ROW_OF = (1, 0, 2, 3, KV_ROW)
-SUM_ROWS = TILES + 4
-
-FIRST = 96
-PIECES = ((0, FIRST), (FIRST, 288), (384, 128))
-CODED = tuple((0, half * HALF + row, rows, half) for half in range(2) for row, rows in PIECES)
+SUM_ROWS = TILES + 5
+
+FIRST = 128
+CODED_TILES = 2
+CODED = (
+    *((0, half * HALF + row, rows, half) for half in range(2) for row, rows in ((0, FIRST), (FIRST, HALF - FIRST))),
+    *((1, half * HALF, HALF, half) for half in range(2)),
+)
 QUARTER = HALF // 2
 UNITS = (
     *CODED,
-    *((tile, half * HALF, HALF, half) for tile in range(1, TILES - 1) for half in range(2)),
+    *((tile, half * HALF, HALF, half) for tile in range(CODED_TILES, TILES - 1) for half in range(2)),
     *((TILES - 1, part * QUARTER, QUARTER, part // 2) for part in range(4)),
     *((TILES, half * HALF, HALF, half) for half in range(2)),
 )
 FIRST_OF = tuple(min(k for k, unit in enumerate(UNITS) if unit[0] == tile) for tile in range(TILES + 1))
 KV_UNITS = (len(UNITS) - 2, len(UNITS) - 1)
-SIDE_GROUPS = ((0, 1, 2), (3, 4, 5), (6, 7, 8, 9), (10, 11, 12, 13, 14, 15))
-FAR_GROUPS = ((0, 1, 2), (3, 4, 5), (6, 8), (7, 9), (10,), (12,), (11,), (13,), (14,), (15,))
+SIDE_GROUPS = ((0, 1), (2, 3), (4, 5, 6, 7), (8, 9, 10, 11, 12, 13))
+FAR_GROUPS = ((0, 1), (2, 3), (4, 6), (5, 7), (8,), (10,), (9,), (11,), (12,), (13,))
 SIDE_OF = {k: g for g, units in enumerate(SIDE_GROUPS) for k in units}
 FAR_OF = {k: g for g, units in enumerate(FAR_GROUPS) for k in units}
 CODE = 180.0
@@ -146,23 +147,28 @@
 
     def sum_rows(t, first, rows, carry):
         cols = pl.ds(t * LANES, LANES)
-        step = STEPS[rows]
 
         def body(i, carry):
             acc, top = carry
-            at = pl.ds(pl.multiple_of(first + i * step, 8), step)
+            at = pl.ds(pl.multiple_of(first + i * STEP, STEP), STEP)
             r = mix(sq_v[at, cols], wq_v[at, cols])
             res_q[at, cols] = r
-            size = jnp.abs(r).reshape(step // 8, 8, LANES)
+            size = jnp.abs(r).reshape(STEP // 8, 8, LANES)
             acc = acc + jnp.sum(size, axis=0)
-            return acc, jnp.maximum(top, jnp.max(size, axis=0)) if t == 0 else top
-
-        return lax.fori_loop(0, rows // step, body, carry)
+            return acc, jnp.maximum(top, jnp.max(size, axis=0)) if t < CODED_TILES else top
+
+        return lax.fori_loop(0, rows // STEP, body, carry)
+
+    def code_scale(top, row):
+        top = jnp.maximum(jnp.max(top, axis=0, keepdims=True), 1e-30)
+        sums[me, MAX_ROW + row] = top
+        return CODE / top
 
     def sum_tile(t):
         wait_bytes(wq_v.at[:, pl.ds(0, 2 * LANES)], in_sem.at[t])
-        acc, _ = sum_rows(t, 0, ROWS, (nothing, nothing))
-        sums[me, ROW_OF[t]] = jnp.sum(acc, axis=0, keepdims=True)
+        acc, top = sum_rows(t, 0, ROWS, (nothing, nothing))
+        sums[me, t] = jnp.sum(acc, axis=0, keepdims=True)
+        return code_scale(top, 2) if t < CODED_TILES else None
 
     def sum_first(part, acc):
         row, rows = (0, FIRST) if part == 0 else (FIRST, HALF - FIRST)
@@ -171,17 +177,15 @@
         for half in range(2):
             carry = sum_rows(0, half * HALF + row, rows, carry)
         acc, top = carry
-        top = jnp.maximum(jnp.max(top, axis=0, keepdims=True), 1e-30)
-        sums[me, MAX_ROW + part] = top
-        return acc, CODE / top
-
-    def send_sums(first, count, which):
+        return acc, code_scale(top, part)
+
+    def send_sums():
         for d in (4, 5, 3, 2, 6, 7, 1):
             pltpu.make_async_remote_copy(
-                src_ref=sums.at[me, pl.ds(first, count)],
-                dst_ref=sums.at[me, pl.ds(first, count)],
+                src_ref=sums.at[me],
+                dst_ref=sums.at[me],
                 send_sem=sum_send,
-                recv_sem=sum_recv.at[which],
+                recv_sem=sum_recv,
                 device_id=group_peer(d),
                 device_id_type=MESH,
             ).start()
@@ -190,7 +194,7 @@
         tile, row, rows, _ = UNITS[k]
         at = (origin * 2 + core) * ROWS + row
         if tile < TILES:
-            return out_q.at[pl.ds(pl.multiple_of(at, 32), rows), pl.ds(tile * LANES, LANES)]
+            return out_q.at[pl.ds(pl.multiple_of(at, STEP), rows), pl.ds(tile * LANES, LANES)]
         return out_kv.at[:, pl.ds(pl.multiple_of(at, HALF), rows)]
 
     def kv_part(origin, k, last):
@@ -199,8 +203,8 @@
         return out_kv.at[:, pl.ds(pl.multiple_of(at, LANES), columns)]
 
     def place(origin, k):
-        _, row, rows, _ = UNITS[k]
-        return coded.at[origin, pl.ds(row, rows)] if k < len(CODED) else final_place(origin, k, c)
+        tile, row, rows, _ = UNITS[k]
+        return coded.at[origin, tile, pl.ds(row, rows)] if k < len(CODED) else final_place(origin, k, c)
 
     def unit_copy(ref, recv_sem, device, sem=send_sem):
         return pltpu.make_async_remote_copy(
@@ -223,51 +227,48 @@
         unit_copy(final_place(origin, k, c), rel_recv, partner).start()
 
     def encode_rows(k, scale):
-        _, row, rows, _ = UNITS[k]
-        step = STEPS[rows]
+        tile, row, rows, _ = UNITS[k]
+        cols = pl.ds(tile * LANES, LANES)
 
         def body(i, carry):
-            at = pl.ds(pl.multiple_of(row + i * step, 16), step)
-            coded[x, at, :] = encode(res_q[at, 0:LANES], scale)
+            at = pl.ds(pl.multiple_of(row + i * STEP, STEP), STEP)
+            coded[x, tile, at, :] = encode(res_q[at, cols], scale)
             return carry
 
-        lax.fori_loop(0, rows // step, body, 0)
-
-    def decode_rows(origin, k, scale):
-        _, row, rows, _ = UNITS[k]
-        step = STEPS[rows]
-        own = sums[origin * 2 + c, MAX_ROW + (k % 3 > 0)] * scale
+        lax.fori_loop(0, rows // STEP, body, 0)
+
+    def decode_rows(origin, k, scales):
+        tile, row, rows, _ = UNITS[k]
+        cols = pl.ds(tile * LANES, LANES)
+        own = sums[origin * 2 + c, MAX_ROW + (2 if tile else int(rows != FIRST))] * scales[tile]
 
         def body(i, carry):
-            at = pl.multiple_of(row + i * step, 16)
-            there = pl.ds(pl.multiple_of((origin * 2 + c) * ROWS + at, 16), step)
-            out_q[there, 0:LANES] = (decode(coded[origin, pl.ds(at, step), :]) * own).astype(jnp.bfloat16)
+            at = pl.multiple_of(row + i * STEP, STEP)
+            there = pl.ds(pl.multiple_of((origin * 2 + c) * ROWS + at, STEP), STEP)
+            out_q[there, cols] = (decode(coded[origin, tile, pl.ds(at, STEP), :]) * own).astype(jnp.bfloat16)
             return carry
 
-        lax.fori_loop(0, rows // step, body, 0)
+        lax.fori_loop(0, rows // STEP, body, 0)
 
     lane_of = lax.broadcasted_iota(jnp.int32, (KV, LANES), 1)
     diagonal = lane_of == lax.broadcasted_iota(jnp.int32, (KV, LANES), 0)
 
     acc, scale = sum_first(0, nothing)
     encode_rows(0, scale)
-    encode_rows(3, scale)
+    encode_rows(2, scale)
     wait_for_neighbours()
     send_right(0)
-    send_left(3)
+    send_left(2)
     acc, scale = sum_first(1, acc)
     encode_rows(1, scale)
     send_right(1)
-    encode_rows(4, scale)
-    send_left(4)
-    sum_tile(1)
-    wait_for_far()
-    send_sums(0, 1, 0)
-    encode_rows(2, scale)
-    send_right(2)
-    encode_rows(5, scale)
-    send_left(5)
-    sums[me, ROW_OF[0]] = jnp.sum(acc, axis=0, keepdims=True)
+    encode_rows(3, scale)
+    for k in (3, 0, 1):
+        send_left(k)
+    for k in (2, 3):
+        send_right(k)
+    sums[me, 0] = jnp.sum(acc, axis=0, keepdims=True)
+    scale = sum_tile(1)
     wait_bytes(wq_v.at[pl.ds(0, 4 * 32 * ROWS // COLS), :], in_sem.at[KV_ROW + 1])
     acc = jnp.zeros((KV, LANES), jnp.float32)
     for j in range(ROWS // LANES):
@@ -282,16 +283,19 @@
     sums[me, NORM_ROW] = jnp.concatenate([own_norm, own_norm], axis=1)
     for t in range(2, TILES):
         sum_tile(t)
-    send_sums(1, SUM_ROWS - 1, 1)
-    for k in (0, 1, 2):
+    wait_for_far()
+    send_sums()
+    encode_rows(4, scale)
+    encode_rows(5, scale)
+    for k in (4, 5):
+        send_right(k)
+    for k in (5, 4):
         send_left(k)
-    for k in (3, 4, 5):
-        send_right(k)
 
     def factor_of(t):
-        total = sums[0, ROW_OF[t]]
+        total = sums[0, t]
         for other in range(1, 8):
-            total = total + sums[other, ROW_OF[t]]
+            total = total + sums[other, t]
         return total * (1.0 / D_MODEL)
 
     def narrow_tile(t):
@@ -327,16 +331,16 @@
                         go_there(k)
                     relay(x, k)
 
-    wait_bytes(sums.at[pl.ds(0, 7), pl.ds(0, 1)], sum_recv.at[0])
-    narrow_tile(1)
-    wait_bytes(sums.at[pl.ds(0, 7), pl.ds(1, SUM_ROWS - 1)], sum_recv.at[1])
-    for t in range(2, TILES + 1):
+    wait_bytes(sums.at[pl.ds(0, 7)], sum_recv)
+    for t in range(CODED_TILES, TILES + 1):
         narrow_tile(t)
-    first_factor = factor_of(0)
-    fac_q[:, 0:LANES] = first_factor
-    first_scale = 1.0 / (CODE * first_factor)
+    scales = []
+    for t in range(CODED_TILES):
+        factor = factor_of(t)
+        fac_q[:, pl.ds(t * LANES, LANES)] = factor
+        scales.append(1.0 / (CODE * factor))
     for k in range(len(CODED)):
-        decode_rows(x, k, first_scale)
+        decode_rows(x, k, scales)
         relay(x, k)
 
     def norm_copy(buf, at, stage, device):
@@ -383,7 +387,7 @@
 
     def hand_on(origin, k):
         if k < len(CODED):
-            decode_rows(origin, k, first_scale)
+            decode_rows(origin, k, scales)
         relay(origin, k)
 
     def forward(origin, k):
@@ -507,7 +511,7 @@
             pltpu.VMEM((KV, ROWS), f32),
             pltpu.VMEM((KV, ROWS), f32),
             pltpu.VMEM((2, 1, 64), f32),
-            pltpu.VMEM((4, ROWS, LANES), bf16),
+            pltpu.VMEM((4, CODED_TILES, ROWS, LANES), bf16),
             pltpu.VMEM((8, SUM_ROWS, 1, LANES), f32),
             pltpu.VMEM((4, 8, LANES), f32),
             pltpu.VMEM((4, 2, 8, LANES), f32),
@@ -516,7 +520,7 @@
             dma,
             dma,
             dma,
-            dma((2,)),
+            dma,
             dma((2, len(SIDE_GROUPS))),
             dma((len(FAR_GROUPS),)),
             dma,

time: 50.4 us -> 50.2 us (level)
  no operation moved by 1% of the time
where the time goes in v8:
time: 50.2 us; the launch traced here: 50.1 us
  Pallas kernels  49.4 us (98%)
  between operations  0.65 us (1%)
    pallas_call x1, Pallas kernels, on_device(): pl.pallas_call(gather_kernel, out_shape=tuple((pltpu.VMEM(shape, dtype) f...  45.1 us
    pallas_call x1, Pallas kernels, on_device(): pl.pallas_call(write_kernel, out_shape=tuple((jax.ShapeDtypeStruct(shape,...  4.38 us

profile of v8, /device:TPU:1, one launch (start us, length us, event | category | flops | bytes accessed | tf_op | source)
XLA Modules:
  0.0 50.1 jit_solution(12845941469514511964)
XLA Ops:
  0.6 45.1 %gather.1 = (bf16[8192,512]{1,0:T(8,128)(2,1)S(1)}, bf16[64,8192]{1,0:T(8,128)(2,1)S(1)}, f32[1024,512]{1,0:T(8,128)S(1)}, f32[64,1024]{1,0:T(8,128)S(1)}, f32[1...) custom-call(f32[1024,512]{1,0:T(8,128)} %wq.1, f32[1024,512]{1,0:T(8,128)} %sq.1, ...), custom_call_target="tpu_custom_call" | custom-call | tf_op jit(solution)/shard_map/gather/pallas_call | solution.py:503
  45.7 4.4 %write.1 = (bf16[8192,512]{1,0:T(8,128)(2,1)}, bf16[32,8192]{1,0:T(8,128)(2,1)}, bf16[32,8192]{1,0:T(8,128)(2,1)}, f32[1,512]{1,0:T(1,128)}, f32[1,32]{1,0:T(1,1...) custom-call(bf16[8192,512]{1,0:T(8,128)(2,1)S(1)} %get-tuple-element, ...), custom_call_target="tpu_custom_call" | custom-call | tf_op jit(solution)/shard_map/write/pallas_call | solution.py:559

commit v9 on v8

--- a/solution.py
+++ b/solution.py
@@ -30,11 +30,11 @@
     *((0, half * HALF + row, rows, half) for half in range(2) for row, rows in ((0, FIRST), (FIRST, HALF - FIRST))),
     *((1, half * HALF, HALF, half) for half in range(2)),
 )
-QUARTER = HALF // 2
+LAST = 128
 UNITS = (
     *CODED,
     *((tile, half * HALF, HALF, half) for tile in range(CODED_TILES, TILES - 1) for half in range(2)),
-    *((TILES - 1, part * QUARTER, QUARTER, part // 2) for part in range(4)),
+    *((TILES - 1, half * HALF + row, rows, half) for half in range(2) for row, rows in ((0, HALF - LAST), (HALF - LAST, LAST))),
     *((TILES, half * HALF, HALF, half) for half in range(2)),
 )
 FIRST_OF = tuple(min(k for k, unit in enumerate(UNITS) if unit[0] == tile) for tile in range(TILES + 1))
@@ -181,14 +181,20 @@
 
     def send_sums():
         for d in (4, 5, 3, 2, 6, 7, 1):
+            same = d % 2 == 0
+            rows = pl.ds(0, SUM_ROWS if same else MAX_ROW)
             pltpu.make_async_remote_copy(
-                src_ref=sums.at[me],
-                dst_ref=sums.at[me],
-                send_sem=sum_send,
-                recv_sem=sum_recv,
+                src_ref=sums.at[me, rows],
+                dst_ref=sums.at[me, rows],
+                send_sem=sum_send.at[int(same)],
+                recv_sem=sum_recv.at[int(same)],
                 device_id=group_peer(d),
                 device_id_type=MESH,
             ).start()
+
+    def wait_sums(sem):
+        wait_bytes(sums.at[pl.ds(0, 4), pl.ds(0, MAX_ROW)], sem.at[0])
+        wait_bytes(sums.at[pl.ds(0, 3)], sem.at[1])
 
     def final_place(origin, k, core):
         tile, row, rows, _ = UNITS[k]
@@ -331,7 +337,7 @@
                         go_there(k)
                     relay(x, k)
 
-    wait_bytes(sums.at[pl.ds(0, 7)], sum_recv)
+    wait_sums(sum_recv)
     for t in range(CODED_TILES, TILES + 1):
         narrow_tile(t)
     scales = []
@@ -450,7 +456,7 @@
     share = ROWS + KV * ROWS // COLS
     kv_rows = KV * ROWS // COLS
 
-    wait_bytes(sums.at[pl.ds(0, 7)], sum_send)
+    wait_sums(sum_send)
 
     @pl.when(c == 1)
     def _():
@@ -519,8 +525,8 @@
             dma((NORM_ROW + 2,)),
             dma,
             dma,
-            dma,
-            dma,
+            dma((2,)),
+            dma((2,)),
             dma((2, len(SIDE_GROUPS))),
             dma((len(FAR_GROUPS),)),
             dma,

time: 50.2 us -> 50.1 us (level)
  no operation moved by 1% of the time
where the time goes in v9:
time: 50.1 us; the launch traced here: 49.9 us
  Pallas kernels  49.3 us (98%)
  between operations  0.65 us (1%)
    pallas_call x1, Pallas kernels, on_device(): pl.pallas_call(gather_kernel, out_shape=tuple((pltpu.VMEM(shape, dtype) f...  44.9 us
    pallas_call x1, Pallas kernels, on_device(): pl.pallas_call(write_kernel, out_shape=tuple((jax.ShapeDtypeStruct(shape,...  4.38 us

profile of v9, /device:TPU:1, one launch (start us, length us, event | category | flops | bytes accessed | tf_op | source)
XLA Modules:
  0.0 49.9 jit_solution(13716190330151112314)
XLA Ops:
  0.6 44.9 %gather.1 = (bf16[8192,512]{1,0:T(8,128)(2,1)S(1)}, bf16[64,8192]{1,0:T(8,128)(2,1)S(1)}, f32[1024,512]{1,0:T(8,128)S(1)}, f32[64,1024]{1,0:T(8,128)S(1)}, f32[1...) custom-call(f32[1024,512]{1,0:T(8,128)} %wq.1, f32[1024,512]{1,0:T(8,128)} %sq.1, ...), custom_call_target="tpu_custom_call" | custom-call | tf_op jit(solution)/shard_map/gather/pallas_call | solution.py:509
  45.6 4.4 %write.1 = (bf16[8192,512]{1,0:T(8,128)(2,1)}, bf16[32,8192]{1,0:T(8,128)(2,1)}, bf16[32,8192]{1,0:T(8,128)(2,1)}, f32[1,512]{1,0:T(1,128)}, f32[1,32]{1,0:T(1,1...) custom-call(bf16[8192,512]{1,0:T(8,128)(2,1)S(1)} %get-tuple-element, ...), custom_call_target="tpu_custom_call" | custom-call | tf_op jit(solution)/shard_map/write/pallas_call | solution.py:565
